TPU v7x, 128 devices: a whole 4x4x4 slice. The times are simulated.
128 devices in a mesh: gx: 4 (over y), gy: 32 (over x, z, core).
Axes of the slice: x: 4, y: 4, z: 4, core: 2. Of those that a mesh axis runs over, the one named last changes fastest.
Arguments:
- element_fields: bfloat16 [65536, 5, 512], P(('gx', 'gy')), may hold values from -6 to 6
- ref_coords: float32 [3, 262144], P(None, ('gx', 'gy')), may hold values from -1 to 1
- local_element: int32 [262144], P(('gx', 'gy')), may hold values from 0 to 511
- owner: int32 [262144, 1], P(('gx', 'gy')), may hold values from 0 to 127; in each aligned block of 2048 rows (0 to 2047, 2048 to 4095, ...) at most 64 rows name the same one
- point_angle: float32 [262144], P(('gx', 'gy')), may hold values from -3.140625 to 3.140625
- point_axial: float32 [262144], P(('gx', 'gy')), may hold values from 0 to 8
- panel_weight: float32 [262144], P(('gx', 'gy')), may hold values from 0.5 to 2
- obs_radius: float32 [256], replicated, may hold values from 3 to 30
- obs_angle: float32 [256], replicated, may hold values from -3.140625 to 3.140625
- obs_axial: float32 [256], replicated, may hold values from -8 to 16
- step_phase: float32 [32], replicated, may hold values from -3.140625 to 3.140625
- observer_slot: int32 [256], replicated, may hold values from 0 to 255, each once
- prior_spectra: float32 [2, 32, 256], P(None, None, ('gx', 'gy')), may hold values from -6 to 6
Outputs:
- surface_values: float32 [5, 262144], P(None, ('gx', 'gy'))
- spectra: float32 [2, 32, 256], P(None, None, ('gx', 'gy'))
Inputs may be any that keep to these rules, and one draw needn't show every extreme that they name: Among the points of one device at most 64 have the same owner, and in every draw some device has exactly 64 points owned by one device. `observer_slot`: each output column is named by exactly one observer.
All inputs are finite; a program needn't handle non-finite values.
Results may differ from a plain program's by a relative error of at most 0.0003.
Values sent between devices are 32-bit elements; how exact they have to be, the bound alone decides.
A program may use at most 64 MiB of HBM per device.

v0:
```python
import math

import jax
import jax.numpy as jnp
import numpy as np
from jax import lax
from jax.sharding import PartitionSpec as P

NODES = 512
FIELDS = 5


gll_nodes = np.array(
    [
        -1.0,
        -0.8717401485096066,
        -0.5917001814331423,
        -0.2092992179024789,
        0.2092992179024789,
        0.5917001814331423,
        0.8717401485096066,
        1.0,
    ]
)
omega_base = 0.25


def cut_along(value, dim, peers):
    dims = value.shape
    tiles = value.reshape(*dims[:dim], peers, dims[dim] // peers, *dims[dim + 1 :])
    return jnp.moveaxis(tiles, dim, 0)


def laid_out(tiles, dim):
    tiles = jnp.moveaxis(tiles, 0, dim)
    dims = tiles.shape
    return tiles.reshape(*dims[:dim], dims[dim] * dims[dim + 1], *dims[dim + 2 :])


def exchange_both(value, axis, axes, splits, concats):
    sizes = [lax.axis_size(a) for a in axes]
    tiles = cut_along(value, splits[0], sizes[0])
    tiles = jnp.moveaxis(cut_along(tiles, splits[1] + 1, sizes[1]), 0, 1)
    inside = tiles.shape[2:]
    tiles = tiles.reshape(-1, *inside)
    tiles = lax.all_to_all(tiles, axis, split_axis=0, concat_axis=0, tiled=True)
    tiles = laid_out(tiles.reshape(*sizes, *inside), concats[0] + 1)
    return laid_out(tiles, concats[1])


def total_of_pieces(value, axis):
    tiles = lax.all_gather(value, axis)
    return tiles.sum(axis=0)


def lagrange(coord):
    columns = []
    for first in range(8):
        product = jnp.ones_like(coord)
        divisor = 1.0
        for second in range(8):
            if second != first:
                product = product * (coord - float(gll_nodes[second]))
                divisor = divisor * (gll_nodes[first] - gll_nodes[second])
        columns.append(product * float(1.0 / divisor))
    return jnp.stack(columns)


def node_weights(coords):
    along_r = lagrange(coords[0])
    along_s = lagrange(coords[1])
    along_t = lagrange(coords[2])
    pair_rs = along_r[:, None, :] * along_s[None, :, :]
    return (pair_rs[:, :, None, :] * along_t[None, None, :, :]).reshape(NODES, coords.shape[1])


def interpolate(fields, elem_ids, coords):
    slot_count = elem_ids.shape[0]
    block_rows = math.gcd(slot_count, 1024)
    block_count = slot_count // block_rows

    def sample(pieces):
        weights = node_weights(pieces[1])
        gathered = jnp.take(fields, pieces[0], axis=0).astype(jnp.float32)
        return jnp.einsum("nfq,qn->fn", gathered, weights)

    sampled = lax.map(
        sample,
        (
            elem_ids.reshape(block_count, block_rows),
            coords.reshape(3, block_count, block_rows).transpose(1, 0, 2),
        ),
    )
    return sampled.transpose(1, 0, 2).reshape(FIELDS, slot_count)


def spectra_terms(
    values, angle, axial, weight, obs_radius, obs_angle, obs_axial, step_phase, norm_scale
):
    cos_p = jnp.cos(angle)
    sin_p = jnp.sin(angle)
    step_x = (obs_radius * jnp.cos(obs_angle))[None, :] - cos_p[:, None]
    step_y = (obs_radius * jnp.sin(obs_angle))[None, :] - sin_p[:, None]
    step_z = obs_axial[None, :] - axial[:, None]
    distance = jnp.sqrt(step_x * step_x + step_y * step_y + step_z * step_z)
    density = values[0]
    vel_x = values[1]
    vel_y = values[2]
    vel_z = values[3]
    pressure = values[4]
    mass_flux = density * (vel_x * cos_p + vel_y * sin_p)
    radial = (step_x * cos_p[:, None] + step_y * sin_p[:, None]) / distance
    radial_vel = (
        vel_x[:, None] * step_x + vel_y[:, None] * step_y + vel_z[:, None] * step_z
    ) / distance
    amplitude = (
        weight[:, None]
        * (mass_flux[:, None] + pressure[:, None] * radial + mass_flux[:, None] * radial_vel)
        * obs_radius[None, :]
        / distance
        * norm_scale
    )
    harmonic = omega_base * jnp.arange(1, step_phase.shape[0] + 1, dtype=jnp.float32)
    phases = distance[:, :, None] * harmonic[None, None, :] + step_phase[None, None, :]
    cos_sum = jnp.sum(amplitude[:, :, None] * jnp.cos(phases), axis=0).T
    sin_sum = -jnp.sum(amplitude[:, :, None] * jnp.sin(phases), axis=0).T
    return jnp.stack([cos_sum, sin_sum])


def on_device(
    element_fields,
    ref_coords,
    local_element,
    owner,
    point_angle,
    point_axial,
    panel_weight,
    obs_radius,
    obs_angle,
    obs_axial,
    step_phase,
    observer_slot,
    prior_spectra,
):
    devices = lax.axis_size(("gx", "gy"))
    points = local_element.shape[0]
    capacity = 4 * points // devices
    target = owner[:, 0]
    rank_rows = math.gcd(points, 512)
    rank_blocks = points // rank_rows
    one_hot = (
        (target[:, None] == jnp.arange(devices, dtype=jnp.int32)[None, :])
        .astype(jnp.bfloat16)
        .reshape(rank_blocks, rank_rows, devices)
    )
    strict_lower = (jnp.arange(rank_rows)[:, None] > jnp.arange(rank_rows)[None, :]).astype(
        jnp.bfloat16
    )
    within = jnp.einsum("ij,bjd->bid", strict_lower, one_hot, preferred_element_type=jnp.float32)
    hot_float = one_hot.astype(jnp.float32)
    totals = jnp.sum(hot_float, axis=1)
    offsets = jnp.cumsum(totals, axis=0) - totals
    slot_rank = (
        jnp.sum(hot_float * (within + offsets[:, None, :]), axis=2)
        .reshape(points)
        .astype(jnp.int32)
    )
    position = target * capacity + slot_rank
    send_ids = jnp.zeros((devices * capacity,), jnp.int32).at[position].set(local_element)
    send_coords = jnp.zeros((3, devices * capacity), jnp.float32).at[:, position].set(ref_coords)
    outer = lax.axis_size("gx")
    inner = lax.axis_size("gy")
    arrived = (
        lax.all_to_all(
            lax.all_to_all(
                send_ids.reshape(1, outer, inner, capacity),
                "gy",
                split_axis=2,
                concat_axis=2,
                tiled=True,
            ),
            "gx",
            split_axis=1,
            concat_axis=1,
            tiled=True,
        ),
        lax.all_to_all(
            lax.all_to_all(
                send_coords.reshape(3, outer, inner, capacity),
                "gy",
                split_axis=2,
                concat_axis=2,
                tiled=True,
            ),
            "gx",
            split_axis=1,
            concat_axis=1,
            tiled=True,
        ),
    )
    elem_ids = arrived[0].reshape(1, devices, capacity)
    coords = arrived[1].reshape(3, devices, capacity)
    slot_count = elem_ids.shape[1] * elem_ids.shape[2]
    interpolated = interpolate(
        element_fields, elem_ids.reshape(slot_count), coords.reshape(3, slot_count)
    )
    served = interpolated.reshape(FIELDS, elem_ids.shape[1], elem_ids.shape[2])
    replies = exchange_both(
        served.reshape(FIELDS, outer, inner, capacity), ("gx", "gy"), ("gx", "gy"), (1, 2), (1, 2)
    )
    surface_values = replies.reshape(FIELDS, devices * capacity)[:, position]
    norm_scale = 1.0 / math.sqrt(points * devices)
    green_rows = math.gcd(points, 256)
    green_blocks = points // green_rows

    def accumulate(running, pieces):
        return (
            running
            + spectra_terms(
                pieces[0],
                pieces[1],
                pieces[2],
                pieces[3],
                obs_radius,
                obs_angle,
                obs_axial,
                step_phase,
                norm_scale,
            ),
            None,
        )

    starting = jnp.zeros((2, step_phase.shape[0], obs_radius.shape[0]), jnp.float32)
    summed, unused = lax.scan(
        accumulate,
        starting,
        (
            surface_values.reshape(FIELDS, green_blocks, green_rows).transpose(1, 0, 2),
            point_angle.reshape(green_blocks, green_rows),
            point_axial.reshape(green_blocks, green_rows),
            panel_weight.reshape(green_blocks, green_rows),
        ),
    )
    placed = jnp.zeros_like(summed).at[:, :, observer_slot].set(summed)
    owned_cols = prior_spectra.shape[2]
    everyone = total_of_pieces(placed, ("gx", "gy"))
    owned_part = lax.dynamic_slice_in_dim(
        everyone, lax.axis_index(("gx", "gy")) * owned_cols, owned_cols, 2
    )
    return (surface_values, prior_spectra + owned_part)


def solution(mesh):
    return jax.shard_map(
        on_device,
        mesh=mesh,
        in_specs=(
            P(("gx", "gy"), None, None),
            P(None, ("gx", "gy")),
            P(("gx", "gy")),
            P(("gx", "gy"), None),
            P(("gx", "gy")),
            P(("gx", "gy")),
            P(("gx", "gy")),
            P(),
            P(),
            P(),
            P(),
            P(),
            P(None, None, ("gx", "gy")),
        ),
        out_specs=(P(None, ("gx", "gy")), P(None, None, ("gx", "gy"))),
        check_vma=False,
    )
```

profile of v0, /device:TPU:1, one launch (start us, length us, event | category | flops | bytes accessed | tf_op | source)
XLA Modules:
  0.0 694.6 jit_solution(8669734870792465096)
XLA Ops:
  10.9 8.2 %scatter_custom_fusion.1 = s32[8192]{0:T(1024)S(1)} fusion(s32[2048]{0:T(1024)S(1)} %bitcast.675, s32[2048]{0:T(1024)} %param.19, s32[]{:T(128)} %constant.211.clone.1), kind=kCustom, calls=%fused_computation.212 | custom fusion | bytes 33280 | tf_op jit(solution)/shard_map/scatter | solution.py:169
  20.0 9.4 %all-to-all-start.2 = ((s32[32,1,256]{2,1,0:T(1,128)}), s32[32,1,256]{2,1,0:T(1,128)S(1)}, u32[]{:S(2)}, u32[]{:S(2)}) async-start(s32[32,1,256]{2,1,0:T(1,128)} %reshape.2290), calls=%async_computation.2 | async-start | bytes 65536 | tf_op jit(solution)/shard_map/all_to_all | solution.py:175
  29.4 2.1 copy.81
  31.6 8.1 %scatter_custom_fusion = f32[3,8192]{0,1:T(8,128)} fusion(s32[2048]{0:T(1024)S(1)} %bitcast.676, f32[2048,3]{1,0:T(8,128)} %copy.81, f32[]{:T(128)} %constant.212.clone.1), kind=kCustom, calls=%fused_computation.199 | custom fusion | bytes 98816 | tf_op jit(solution)/shard_map/scatter | solution.py:170
  39.7 3.0 copy.82
  43.5 7.4 %all-to-all-start = ((f32[32,1,768]{2,1,0:T(1,128)}), f32[32,1,768]{2,1,0:T(1,128)S(1)}, u32[]{:S(2)}, u32[]{:S(2)}) async-start(f32[32,1,768]{2,1,0:T(1,128)} %reshape.2286), calls=%async_computation | async-start | bytes 196608 | tf_op jit(solution)/shard_map/all_to_all | solution.py:188
  52.9 5.4 all-to-all-done
  58.3 4.2 all-to-all-start.3
  64.9 1.9 all-to-all-done.3
  66.8 3.5 all-to-all-start.1
  70.4 3.6 copy.88
  76.1 246.7 %while.26 = (s32[]{:T(128)}, f32[8,5,1024]{2,1,0:T(8,128)S(1)}, f32[8,3,1024]{2,0,1:T(8,128)S(1)}, s32[8,1024]{1,0:T(8,128)S(1)}, bf16[512,5,512]{2,1,0:T(8,128)(2,1)}, /*index=5*/s32[]{:T(128)}, s32[]{:T(128)}, s32[]{}, s32[]{}) while((s32[]{:T(128)}, f32[8,5,1024]{2,1,0:T(8,128)S(1)}, f32[8,3,1024]{2,0,1:T(8,128)S(1)}, ...), condition=%wide.region_6.7_spmd, body=%wide.region_5.6_spmd.sunk | while | flops 11257860 | bytes 33630388 | solution.py:87
  76.9 1.9 copy.123
  78.8 12.0 %gather_fusion = bf16[1024,5,512]{2,1,0:T(8,128)(2,1)} fusion(bf16[512,5,512]{2,1,0:T(8,128)(2,1)} %get-tuple-element.618, s32[1024]{0:T(1024)S(1)} %broadcast_clamp_fusion.3), kind=kCustom, calls=%fused_computation.clone.1 | custom fusion | bytes 10489856 | tf_op jit(solution)/shard_map/while/body/eval_jaxpr/jit(_take)/gather | solution.py:84
  90.8 15.9 %multiply_reduce_fusion.5 = f32[1024,5]{1,0:T(8,128)S(1)} fusion(f32[1024,512]{1,0:T(8,128)S(1)} %copy-done, bf16[1024,5,512]{2,1,0:T(8,128)(2,1)} %gather_fusion, pred[1024]{0:T(1024)(128)(4,1)S(1)} %compare_and_fusion.2), kind=kLoop, calls=%fused_computation.46.clone.1 | loop fusion | flops 10480640 | bytes 7361536 | tf_op jit(solution)/shard_map/while
  107.7 1.9 copy.123
  109.6 12.0 %gather_fusion = bf16[1024,5,512]{2,1,0:T(8,128)(2,1)} fusion(bf16[512,5,512]{2,1,0:T(8,128)(2,1)} %get-tuple-element.618, s32[1024]{0:T(1024)S(1)} %broadcast_clamp_fusion.3), kind=kCustom, calls=%fused_computation.clone.1 | custom fusion | bytes 10489856 | tf_op jit(solution)/shard_map/while/body/eval_jaxpr/jit(_take)/gather | solution.py:84
  121.6 15.9 %multiply_reduce_fusion.5 = f32[1024,5]{1,0:T(8,128)S(1)} fusion(f32[1024,512]{1,0:T(8,128)S(1)} %copy-done, bf16[1024,5,512]{2,1,0:T(8,128)(2,1)} %gather_fusion, pred[1024]{0:T(1024)(128)(4,1)S(1)} %compare_and_fusion.2), kind=kLoop, calls=%fused_computation.46.clone.1 | loop fusion | flops 10480640 | bytes 7361536 | tf_op jit(solution)/shard_map/while
  138.6 1.9 copy.123
  140.5 12.0 %gather_fusion = bf16[1024,5,512]{2,1,0:T(8,128)(2,1)} fusion(bf16[512,5,512]{2,1,0:T(8,128)(2,1)} %get-tuple-element.618, s32[1024]{0:T(1024)S(1)} %broadcast_clamp_fusion.3), kind=kCustom, calls=%fused_computation.clone.1 | custom fusion | bytes 10489856 | tf_op jit(solution)/shard_map/while/body/eval_jaxpr/jit(_take)/gather | solution.py:84
  152.5 15.9 %multiply_reduce_fusion.5 = f32[1024,5]{1,0:T(8,128)S(1)} fusion(f32[1024,512]{1,0:T(8,128)S(1)} %copy-done, bf16[1024,5,512]{2,1,0:T(8,128)(2,1)} %gather_fusion, pred[1024]{0:T(1024)(128)(4,1)S(1)} %compare_and_fusion.2), kind=kLoop, calls=%fused_computation.46.clone.1 | loop fusion | flops 10480640 | bytes 7361536 | tf_op jit(solution)/shard_map/while
  171.3 12.0 %gather_fusion = bf16[1024,5,512]{2,1,0:T(8,128)(2,1)} fusion(bf16[512,5,512]{2,1,0:T(8,128)(2,1)} %get-tuple-element.618, s32[1024]{0:T(1024)S(1)} %broadcast_clamp_fusion.3), kind=kCustom, calls=%fused_computation.clone.1 | custom fusion | bytes 10489856 | tf_op jit(solution)/shard_map/while/body/eval_jaxpr/jit(_take)/gather | solution.py:84
  183.3 15.9 %multiply_reduce_fusion.5 = f32[1024,5]{1,0:T(8,128)S(1)} fusion(f32[1024,512]{1,0:T(8,128)S(1)} %copy-done, bf16[1024,5,512]{2,1,0:T(8,128)(2,1)} %gather_fusion, pred[1024]{0:T(1024)(128)(4,1)S(1)} %compare_and_fusion.2), kind=kLoop, calls=%fused_computation.46.clone.1 | loop fusion | flops 10480640 | bytes 7361536 | tf_op jit(solution)/shard_map/while
  202.1 12.0 %gather_fusion = bf16[1024,5,512]{2,1,0:T(8,128)(2,1)} fusion(bf16[512,5,512]{2,1,0:T(8,128)(2,1)} %get-tuple-element.618, s32[1024]{0:T(1024)S(1)} %broadcast_clamp_fusion.3), kind=kCustom, calls=%fused_computation.clone.1 | custom fusion | bytes 10489856 | tf_op jit(solution)/shard_map/while/body/eval_jaxpr/jit(_take)/gather | solution.py:84
  214.2 15.9 %multiply_reduce_fusion.5 = f32[1024,5]{1,0:T(8,128)S(1)} fusion(f32[1024,512]{1,0:T(8,128)S(1)} %copy-done, bf16[1024,5,512]{2,1,0:T(8,128)(2,1)} %gather_fusion, pred[1024]{0:T(1024)(128)(4,1)S(1)} %compare_and_fusion.2), kind=kLoop, calls=%fused_computation.46.clone.1 | loop fusion | flops 10480640 | bytes 7361536 | tf_op jit(solution)/shard_map/while
  233.0 12.0 %gather_fusion = bf16[1024,5,512]{2,1,0:T(8,128)(2,1)} fusion(bf16[512,5,512]{2,1,0:T(8,128)(2,1)} %get-tuple-element.618, s32[1024]{0:T(1024)S(1)} %broadcast_clamp_fusion.3), kind=kCustom, calls=%fused_computation.clone.1 | custom fusion | bytes 10489856 | tf_op jit(solution)/shard_map/while/body/eval_jaxpr/jit(_take)/gather | solution.py:84
  245.0 15.9 %multiply_reduce_fusion.5 = f32[1024,5]{1,0:T(8,128)S(1)} fusion(f32[1024,512]{1,0:T(8,128)S(1)} %copy-done, bf16[1024,5,512]{2,1,0:T(8,128)(2,1)} %gather_fusion, pred[1024]{0:T(1024)(128)(4,1)S(1)} %compare_and_fusion.2), kind=kLoop, calls=%fused_computation.46.clone.1 | loop fusion | flops 10480640 | bytes 7361536 | tf_op jit(solution)/shard_map/while
  261.9 1.9 copy.123
  263.8 12.0 %gather_fusion = bf16[1024,5,512]{2,1,0:T(8,128)(2,1)} fusion(bf16[512,5,512]{2,1,0:T(8,128)(2,1)} %get-tuple-element.618, s32[1024]{0:T(1024)S(1)} %broadcast_clamp_fusion.3), kind=kCustom, calls=%fused_computation.clone.1 | custom fusion | bytes 10489856 | tf_op jit(solution)/shard_map/while/body/eval_jaxpr/jit(_take)/gather | solution.py:84
  275.8 15.9 %multiply_reduce_fusion.5 = f32[1024,5]{1,0:T(8,128)S(1)} fusion(f32[1024,512]{1,0:T(8,128)S(1)} %copy-done, bf16[1024,5,512]{2,1,0:T(8,128)(2,1)} %gather_fusion, pred[1024]{0:T(1024)(128)(4,1)S(1)} %compare_and_fusion.2), kind=kLoop, calls=%fused_computation.46.clone.1 | loop fusion | flops 10480640 | bytes 7361536 | tf_op jit(solution)/shard_map/while
  294.6 12.0 %gather_fusion = bf16[1024,5,512]{2,1,0:T(8,128)(2,1)} fusion(bf16[512,5,512]{2,1,0:T(8,128)(2,1)} %get-tuple-element.618, s32[1024]{0:T(1024)S(1)} %broadcast_clamp_fusion.3), kind=kCustom, calls=%fused_computation.clone.1 | custom fusion | bytes 10489856 | tf_op jit(solution)/shard_map/while/body/eval_jaxpr/jit(_take)/gather | solution.py:84
  306.7 15.9 %multiply_reduce_fusion.5 = f32[1024,5]{1,0:T(8,128)S(1)} fusion(f32[1024,512]{1,0:T(8,128)S(1)} %copy-done, bf16[1024,5,512]{2,1,0:T(8,128)(2,1)} %gather_fusion, pred[1024]{0:T(1024)(128)(4,1)S(1)} %compare_and_fusion.2), kind=kLoop, calls=%fused_computation.46.clone.1 | loop fusion | flops 10480640 | bytes 7361536 | tf_op jit(solution)/shard_map/while
  324.8 7.3 %all-to-all-start.4 = ((f32[128,1,320]{2,1,0:T(1,128)}), f32[128,1,320]{2,1,0:T(1,128)S(1)}, u32[]{:S(2)}, u32[]{:S(2)}) async-start(f32[128,1,320]{2,1,0:T(1,128)} %reshape.2294), calls=%async_computation.4 | async-start | bytes 393216 | tf_op jit(solution)/shard_map/all_to_all | solution.py:46
  332.5 10.0 %all-to-all-done.4 = f32[128,1,320]{2,1,0:T(1,128)S(1)} async-done(((f32[128,1,320]{2,1,0:T(1,128)}), f32[128,1,320]{2,1,0:T(1,128)S(1)}, u32[]{:S(2)}, u32[]{:S(2)}) %all-to-all-start.4) | async-done | bytes 163872 | tf_op jit(solution)/shard_map/all_to_all | solution.py:46
  343.9 3.3 copy.91
  347.3 7.6 %gather_fusion.1 = f32[2048,5]{1,0:T(8,128)S(1)} fusion(f32[5,8192]{0,1:T(8,128)} %bitcast.637, s32[2048]{0:T(1024)S(1)} %broadcast_clamp_fusion.1), kind=kCustom, calls=%fused_computation.1 | custom fusion | bytes 90112 | tf_op jit(solution)/shard_map/gather | solution.py:211
  355.2 253.6 %while.27 = (s32[]{:T(128)}, f32[2,32,256]{2,1,0:T(8,128)S(1)}, f32[8,256]{1,0:T(8,128)S(1)}, f32[8,5,256]{2,1,0:T(8,128)S(1)}, f32[8,256]{1,0:T(8,128)S(1)}, /*...) while((s32[]{:T(128)}, f32[2,32,256]{2,1,0:T(8,128)S(1)}, ...), condition=%wide.region_10.11_spmd.clone, body=%wide.region_7.10_spmd.clone.sunk | while | flops 14328903 | bytes 1413747 | solution.py:234
  355.8 31.1 %multiply_reduce_fusion.6 = (f32[256,32]{0,1:T(8,128)S(1)}, f32[256,32]{0,1:T(8,128)S(1)}) fusion(f32[32]{0:T(128)S(1)} %get-tuple-element.667, f32[32]{0:T(128)S(1)} %add_multiply_fusion.4, f32[256,256]{1,0:T(8,128)S(1)} %get-tuple-element.592, f32[256,256]{1,0:T(8,128)S(1)} %get-tuple-element.593), kind=kLoop, calls=%fused_computation.6.clone.1 | loop fusion | flops 12566528 | bytes 590080 | tf_op jit(solution)/shard_map/while/body/eval_jaxpr/reduce_sum | solution.py:125
  387.5 31.1 %multiply_reduce_fusion.6 = (f32[256,32]{0,1:T(8,128)S(1)}, f32[256,32]{0,1:T(8,128)S(1)}) fusion(f32[32]{0:T(128)S(1)} %get-tuple-element.667, f32[32]{0:T(128)S(1)} %add_multiply_fusion.4, f32[256,256]{1,0:T(8,128)S(1)} %get-tuple-element.592, f32[256,256]{1,0:T(8,128)S(1)} %get-tuple-element.593), kind=kLoop, calls=%fused_computation.6.clone.1 | loop fusion | flops 12566528 | bytes 590080 | tf_op jit(solution)/shard_map/while/body/eval_jaxpr/reduce_sum | solution.py:125
  419.2 31.1 %multiply_reduce_fusion.6 = (f32[256,32]{0,1:T(8,128)S(1)}, f32[256,32]{0,1:T(8,128)S(1)}) fusion(f32[32]{0:T(128)S(1)} %get-tuple-element.667, f32[32]{0:T(128)S(1)} %add_multiply_fusion.4, f32[256,256]{1,0:T(8,128)S(1)} %get-tuple-element.592, f32[256,256]{1,0:T(8,128)S(1)} %get-tuple-element.593), kind=kLoop, calls=%fused_computation.6.clone.1 | loop fusion | flops 12566528 | bytes 590080 | tf_op jit(solution)/shard_map/while/body/eval_jaxpr/reduce_sum | solution.py:125
  450.9 31.1 %multiply_reduce_fusion.6 = (f32[256,32]{0,1:T(8,128)S(1)}, f32[256,32]{0,1:T(8,128)S(1)}) fusion(f32[32]{0:T(128)S(1)} %get-tuple-element.667, f32[32]{0:T(128)S(1)} %add_multiply_fusion.4, f32[256,256]{1,0:T(8,128)S(1)} %get-tuple-element.592, f32[256,256]{1,0:T(8,128)S(1)} %get-tuple-element.593), kind=kLoop, calls=%fused_computation.6.clone.1 | loop fusion | flops 12566528 | bytes 590080 | tf_op jit(solution)/shard_map/while/body/eval_jaxpr/reduce_sum | solution.py:125
  482.6 31.1 %multiply_reduce_fusion.6 = (f32[256,32]{0,1:T(8,128)S(1)}, f32[256,32]{0,1:T(8,128)S(1)}) fusion(f32[32]{0:T(128)S(1)} %get-tuple-element.667, f32[32]{0:T(128)S(1)} %add_multiply_fusion.4, f32[256,256]{1,0:T(8,128)S(1)} %get-tuple-element.592, f32[256,256]{1,0:T(8,128)S(1)} %get-tuple-element.593), kind=kLoop, calls=%fused_computation.6.clone.1 | loop fusion | flops 12566528 | bytes 590080 | tf_op jit(solution)/shard_map/while/body/eval_jaxpr/reduce_sum | solution.py:125
  514.3 31.1 %multiply_reduce_fusion.6 = (f32[256,32]{0,1:T(8,128)S(1)}, f32[256,32]{0,1:T(8,128)S(1)}) fusion(f32[32]{0:T(128)S(1)} %get-tuple-element.667, f32[32]{0:T(128)S(1)} %add_multiply_fusion.4, f32[256,256]{1,0:T(8,128)S(1)} %get-tuple-element.592, f32[256,256]{1,0:T(8,128)S(1)} %get-tuple-element.593), kind=kLoop, calls=%fused_computation.6.clone.1 | loop fusion | flops 12566528 | bytes 590080 | tf_op jit(solution)/shard_map/while/body/eval_jaxpr/reduce_sum | solution.py:125
  546.0 31.1 %multiply_reduce_fusion.6 = (f32[256,32]{0,1:T(8,128)S(1)}, f32[256,32]{0,1:T(8,128)S(1)}) fusion(f32[32]{0:T(128)S(1)} %get-tuple-element.667, f32[32]{0:T(128)S(1)} %add_multiply_fusion.4, f32[256,256]{1,0:T(8,128)S(1)} %get-tuple-element.592, f32[256,256]{1,0:T(8,128)S(1)} %get-tuple-element.593), kind=kLoop, calls=%fused_computation.6.clone.1 | loop fusion | flops 12566528 | bytes 590080 | tf_op jit(solution)/shard_map/while/body/eval_jaxpr/reduce_sum | solution.py:125
  577.6 31.1 %multiply_reduce_fusion.6 = (f32[256,32]{0,1:T(8,128)S(1)}, f32[256,32]{0,1:T(8,128)S(1)}) fusion(f32[32]{0:T(128)S(1)} %get-tuple-element.667, f32[32]{0:T(128)S(1)} %add_multiply_fusion.4, f32[256,256]{1,0:T(8,128)S(1)} %get-tuple-element.592, f32[256,256]{1,0:T(8,128)S(1)} %get-tuple-element.593), kind=kLoop, calls=%fused_computation.6.clone.1 | loop fusion | flops 12566528 | bytes 590080 | tf_op jit(solution)/shard_map/while/body/eval_jaxpr/reduce_sum | solution.py:125
  609.1 7.0 %scatter_fusion = f32[2,32,256]{1,0,2:T(2,128)S(1)} fusion(f32[2,32,256]{1,0,2:T(2,128)S(1)} %broadcast.2159, s32[256]{0:T(256)S(1)} %compare_select_fusion.3, f32[256,2,32]{2,1,0:T(2,128)S(1)} %copy.93), kind=kCustom, calls=%fused_computation.4 | custom fusion | bytes 197632 | tf_op jit(solution)/shard_map/scatter | solution.py:244
  617.8 65.4 %all-gather.3.cloned.1.call-done = f32[256,32,256]{2,1,0:T(8,128)} async-done(((f32[2,32,256]{2,1,0:T(8,128)}), f32[256,32,256]{2,1,0:T(8,128)}) %all-gather.3.cloned.1.call-update) | async-done | bytes 8388624 | tf_op jit(solution)/shard_map/all_gather | solution.py:52
  683.1 3.9 reduce_sum.51
  (267 shorter events, 37.9 us)
Async XLA Ops:
  7.2 63.1 %copy-start.2 = (f32[256]{0:T(256)S(1)}, f32[256]{0:T(256)}, u32[]{:S(2)}) copy-start(f32[256]{0:T(256)} %param.24) | copy-start | bytes 3076
  7.2 63.1 %copy-start.9 = (f32[256]{0:T(256)S(1)}, f32[256]{0:T(256)}, u32[]{:S(2)}) copy-start(f32[256]{0:T(256)} %param.25) | copy-start | bytes 3076
  7.2 63.2 %copy-start.1 = (bf16[512,5,512]{2,0,1:T(8,128)(2,1)S(1)}, bf16[512,5,512]{2,0,1:T(8,128)(2,1)}, u32[]{:S(2)}) copy-start(bf16[512,5,512]{2,0,1:T(8,128)(2,1)} %param.17) | copy-start | bytes 7864324
  20.0 23.4 %all-to-all-start.2 = ((s32[32,1,256]{2,1,0:T(1,128)}), s32[32,1,256]{2,1,0:T(1,128)S(1)}, u32[]{:S(2)}, u32[]{:S(2)}) async-start(s32[32,1,256]{2,1,0:T(1,128)} %reshape.2290), calls=%async_computation.2 | async-start | bytes 65536 | tf_op jit(solution)/shard_map/all_to_all | solution.py:175
  31.6 42.4 %copy-start.4 = (f32[2048]{0:T(1024)S(1)}, f32[2048]{0:T(1024)}, u32[]{:S(2)}) copy-start(f32[2048]{0:T(1024)} %param.23) | copy-start | bytes 24580
  31.6 42.4 %copy-start.5 = (f32[2048]{0:T(1024)S(1)}, f32[2048]{0:T(1024)}, u32[]{:S(2)}) copy-start(f32[2048]{0:T(1024)} %param.21) | copy-start | bytes 24580
  31.6 42.4 %copy-start.6 = (f32[2048]{0:T(1024)S(1)}, f32[2048]{0:T(1024)}, u32[]{:S(2)}) copy-start(f32[2048]{0:T(1024)} %param.22) | copy-start | bytes 24580
  43.5 14.8 %all-to-all-start = ((f32[32,1,768]{2,1,0:T(1,128)}), f32[32,1,768]{2,1,0:T(1,128)S(1)}, u32[]{:S(2)}, u32[]{:S(2)}) async-start(f32[32,1,768]{2,1,0:T(1,128)} %reshape.2286), calls=%async_computation | async-start | bytes 196608 | tf_op jit(solution)/shard_map/all_to_all | solution.py:188
  58.3 8.5 %all-to-all-start.3 = ((s32[4,1,2048]{2,1,0:T(1,128)}), s32[4,1,2048]{2,1,0:T(1,128)S(1)}, u32[]{:S(2)}, u32[]{:S(2)}) async-start(s32[4,1,2048]{2,1,0:T(1,128)} %reshape.2292), calls=%async_computation.3 | async-start | bytes 65536 | tf_op jit(solution)/shard_map/all_to_all | solution.py:174
  66.8 8.1 %all-to-all-start.1 = ((f32[4,1,6144]{2,1,0:T(1,128)}), f32[4,1,6144]{2,1,0:T(1,128)S(1)}, u32[]{:S(2)}, u32[]{:S(2)}) async-start(f32[4,1,6144]{2,1,0:T(1,128)} %reshape.2288), calls=%async_computation.1 | async-start | bytes 196608 | tf_op jit(solution)/shard_map/all_to_all | solution.py:187
  76.1 256.4 %copy-start.8 = (s32[256]{0:T(256)S(1)}, s32[256]{0:T(256)}, u32[]{:S(2)}) copy-start(s32[256]{0:T(256)} %param.28) | copy-start | bytes 3076
  78.8 12.0 %copy-start = (f32[1024,512]{1,0:T(8,128)S(1)}, f32[1024,512]{1,0:T(8,128)}, u32[]{:S(2)}) copy-start(f32[1024,512]{1,0:T(8,128)} %copy.123) | copy-start | bytes 6291460 | tf_op jit(solution)/shard_map/while
  109.6 12.0 %copy-start = (f32[1024,512]{1,0:T(8,128)S(1)}, f32[1024,512]{1,0:T(8,128)}, u32[]{:S(2)}) copy-start(f32[1024,512]{1,0:T(8,128)} %copy.123) | copy-start | bytes 6291460 | tf_op jit(solution)/shard_map/while
  140.4 12.0 %copy-start = (f32[1024,512]{1,0:T(8,128)S(1)}, f32[1024,512]{1,0:T(8,128)}, u32[]{:S(2)}) copy-start(f32[1024,512]{1,0:T(8,128)} %copy.123) | copy-start | bytes 6291460 | tf_op jit(solution)/shard_map/while
  171.3 12.0 %copy-start = (f32[1024,512]{1,0:T(8,128)S(1)}, f32[1024,512]{1,0:T(8,128)}, u32[]{:S(2)}) copy-start(f32[1024,512]{1,0:T(8,128)} %copy.123) | copy-start | bytes 6291460 | tf_op jit(solution)/shard_map/while
  202.1 12.0 %copy-start = (f32[1024,512]{1,0:T(8,128)S(1)}, f32[1024,512]{1,0:T(8,128)}, u32[]{:S(2)}) copy-start(f32[1024,512]{1,0:T(8,128)} %copy.123) | copy-start | bytes 6291460 | tf_op jit(solution)/shard_map/while
  233.0 12.0 %copy-start = (f32[1024,512]{1,0:T(8,128)S(1)}, f32[1024,512]{1,0:T(8,128)}, u32[]{:S(2)}) copy-start(f32[1024,512]{1,0:T(8,128)} %copy.123) | copy-start | bytes 6291460 | tf_op jit(solution)/shard_map/while
  263.8 12.0 %copy-start = (f32[1024,512]{1,0:T(8,128)S(1)}, f32[1024,512]{1,0:T(8,128)}, u32[]{:S(2)}) copy-start(f32[1024,512]{1,0:T(8,128)} %copy.123) | copy-start | bytes 6291460 | tf_op jit(solution)/shard_map/while
  294.6 12.0 %copy-start = (f32[1024,512]{1,0:T(8,128)S(1)}, f32[1024,512]{1,0:T(8,128)}, u32[]{:S(2)}) copy-start(f32[1024,512]{1,0:T(8,128)} %copy.123) | copy-start | bytes 6291460 | tf_op jit(solution)/shard_map/while
  322.8 32.5 %copy-start.3 = (f32[256]{0:T(256)S(1)}, f32[256]{0:T(256)}, u32[]{:S(2)}) copy-start(f32[256]{0:T(256)} %param.26) | copy-start | bytes 3076
  322.8 32.5 %copy-start.10 = (f32[32]{0:T(128)S(1)}, f32[32]{0:T(128)}, u32[]{:S(2)}) copy-start(f32[32]{0:T(128)} %param.27) | copy-start | bytes 388
  324.8 17.7 %all-to-all-start.4 = ((f32[128,1,320]{2,1,0:T(1,128)}), f32[128,1,320]{2,1,0:T(1,128)S(1)}, u32[]{:S(2)}, u32[]{:S(2)}) async-start(f32[128,1,320]{2,1,0:T(1,128)} %reshape.2294), calls=%async_computation.4 | async-start | bytes 393216 | tf_op jit(solution)/shard_map/all_to_all | solution.py:46
  332.2 351.0 %all-gather.3.cloned.1.call-start = ((), (), s32[]{:S(2)}) async-start(), calls=%async_computation.5 | async-start | bytes 8454144 | tf_op jit(solution)/shard_map/all_gather | solution.py:52
  608.8 78.4 %copy-start.7 = (f32[2,32,2]{1,2,0:T(2,128)S(1)}, f32[2,32,2]{1,2,0:T(2,128)}, u32[]{:S(2)}) copy-start(f32[2,32,2]{1,2,0:T(2,128)} %param.29) | copy-start | bytes 1540
Sparse Core Ops, SparseCore 0:
  616.9 66.1 all-gather.2
where the time goes:
time: 695 us
  other arithmetic  396 us (57%)
  local copies, waits for them, and re-layouts  168 us (24%)
  waiting for transfers between devices  82.7 us (12%)
  starting transfers between devices  32.1 us (5%)
  between operations  14.4 us (2%)
    reduce_sum x8, other arithmetic, spectra_terms(): cos_sum = jnp.sum(amplitude[:, :, None] * jnp.cos(phases), axis=0).T  249 us
    while x8, other arithmetic  127 us
    gather x8, local copies, waits for them, and re-layouts, sample(): gathered = jnp.take(fields, pieces[0], axis=0).astype(jnp.float32)  96.1 us
    all_gather x1, waiting for transfers between devices, total_of_pieces(): tiles = lax.all_gather(value, axis)  65.4 us
    while x24, local copies, waits for them, and re-layouts  14.9 us
  transfers between devices with their start and end apart: 6, of which 4 were waited for; matrix products, arithmetic and copies ran while one was open for 3% of the time, Pallas kernels for 0%

commit v1 on v0

v1 whole, which is shorter than its diff:
```python
import math

import jax
import jax.numpy as jnp
import numpy as np
from jax import lax
from jax.experimental import pallas as pl
from jax.experimental.pallas import tpu as pltpu
from jax.sharding import PartitionSpec as P

MESH = pl.DeviceIdType.MESH
F32 = jnp.float32
BF16 = jnp.bfloat16

DEV = 128
INNER = 32
CAP = 64
PTS = 2048
ELEM = 512
NODES = 512
FIELDS = 5
NOBS = 256
NFREQ = 32
BLK = 256

GLL = [
    -1.0,
    -0.8717401485096066,
    -0.5917001814331423,
    -0.2092992179024789,
    0.2092992179024789,
    0.5917001814331423,
    0.8717401485096066,
    1.0,
]
CENTRES = ((3, 2), (10, 4), (19, 4), (28, 4))


def fit_sincos():
    r = np.cos((np.arange(400) + 0.5) * np.pi / 400) * (np.pi / 2)
    x = r * r
    cheb = np.polynomial.chebyshev
    top = (np.pi / 2) ** 2

    def poly(y, degree):
        fitted = cheb.Chebyshev.fit(x, y, degree, domain=[0, top])
        return [float(v) for v in fitted.convert(kind=np.polynomial.Polynomial).coef]

    return poly(np.sin(r) / r, 5), poly(np.cos(r), 5)


SIN_C, COS_C = fit_sincos()
PI_HI = 3.140625
PI_LO = math.pi - 3.140625


def horner(coefs, x):
    total = coefs[-1] * x + coefs[-2]
    for value in coefs[-3::-1]:
        total = total * x + value
    return total


def sincos_twice(r):
    x = r * r
    s = horner(SIN_C, x) * r
    c = horner(COS_C, x)
    t = s + s
    return 1.0 - t * s, t * c


def lagrange(coord):
    gaps = [coord - node for node in GLL]
    left = [None, gaps[0]]
    for i in range(2, 8):
        left.append(left[-1] * gaps[i - 1])
    right = [None] * 8
    right[6] = gaps[7]
    for i in range(5, -1, -1):
        right[i] = right[i + 1] * gaps[i + 1]
    values = []
    for i in range(8):
        divisor = 1.0
        for m in range(8):
            if m != i:
                divisor *= GLL[i] - GLL[m]
        scale = float(1.0 / divisor)
        if i == 0:
            product = right[0]
        elif i == 7:
            product = left[7]
        else:
            product = left[i] * right[i]
        values.append(product * scale)
    return values


def split2(x):
    hi = x.astype(BF16)
    lo = (x - hi.astype(F32)).astype(BF16)
    return hi, lo


def split3(x):
    hi = x.astype(BF16)
    rest = x - hi.astype(F32)
    mid = rest.astype(BF16)
    lo = (rest - mid.astype(F32)).astype(BF16)
    return hi, mid, lo


def dot_nt(a, b):
    return lax.dot_general(a, b, (((1,), (1,)), ((), ())), preferred_element_type=F32)


def dot_nn(a, b):
    return lax.dot_general(a, b, (((1,), (0,)), ((), ())), preferred_element_type=F32)


def kernel(
    tab_hbm,
    coords_ref,
    local_ref,
    owner_ref,
    angle_ref,
    axial_ref,
    weight_ref,
    orad_ref,
    oang_ref,
    oax_ref,
    phase_ref,
    slot_ref,
    prior_ref,
    surf_ref,
    spec_ref,
    tab,
    tabt,
    hot,
    rankm,
    req_out,
    req_in,
    rid,
    lag,
    valt,
    rep_out,
    rep_in,
    cols,
    coefs,
    amp,
    inv_ref,
    ys,
    xs,
    sums,
    red_out,
    red_in,
    tab_sem,
    sems,
):
    me = lax.axis_index("gx") * INNER + lax.axis_index("gy")

    def target(d):
        flat = lax.rem(me + d, DEV)
        return flat, (flat // INNER, lax.rem(flat, INNER))

    tab_copy = pltpu.make_async_copy(tab_hbm, tab, tab_sem)
    tab_copy.start()
    barrier = pltpu.get_barrier_semaphore()

    @pl.loop(1, DEV)
    def _(d):
        flat, where = target(d)
        pl.semaphore_signal(barrier, inc=1, device_id=where, device_id_type=MESH)

    def exchange(source, landing, k, own, back=False):
        @pl.loop(1, DEV)
        def _(d):
            flat, where = target(DEV - d if back else d)
            pltpu.make_async_remote_copy(
                src_ref=source.at[flat if own else d],
                dst_ref=landing.at[d],
                send_sem=sems.at[2 * k],
                recv_sem=sems.at[2 * k + 1],
                device_id=where,
                device_id_type=MESH,
            ).start()

    def whole(landing, k):
        rest = landing.at[pl.ds(1, DEV - 1)]
        flat, where = target(1)
        return pltpu.make_async_remote_copy(
            src_ref=rest,
            dst_ref=rest,
            send_sem=sems.at[2 * k],
            recv_sem=sems.at[2 * k + 1],
            device_id=where,
            device_id_type=MESH,
        )

    rel = owner_ref[...] - me
    rel = jnp.where(rel < 0, rel + DEV, rel)
    dev_iota = lax.broadcasted_iota(jnp.int32, (DEV, BLK), 0)
    cap_iota = lax.broadcasted_iota(jnp.int32, (CAP, BLK), 0)
    before = jnp.where(
        lax.broadcasted_iota(jnp.int32, (BLK, BLK), 0) < lax.broadcasted_iota(jnp.int32, (BLK, BLK), 1),
        1.0,
        0.0,
    ).astype(BF16)
    offset = jnp.zeros((DEV, 1), F32)
    packed = jnp.zeros((DEV, 4 * CAP), F32)
    for blk in range(PTS // BLK):
        at = slice(blk * BLK, (blk + 1) * BLK)
        onehot = jnp.where(dev_iota == rel[:, at], 1.0, 0.0)
        onehot16 = onehot.astype(BF16)
        hot[0:DEV, at] = onehot16
        hot[DEV : 2 * DEV, at] = onehot16
        within = dot_nn(onehot16, before)
        rank = jnp.sum(onehot * (within + offset), axis=0, keepdims=True)
        offset = offset + jnp.sum(onehot, axis=1, keepdims=True)
        mask = cap_iota == rank.astype(jnp.int32)
        rankm[:, at] = jnp.where(mask, 1.0, 0.0)
        rows = [local_ref[:, at].astype(F32)] + [coords_ref[v : v + 1, at] for v in range(3)]
        pieces = [split3(row) for row in rows]
        for part in range(3):
            table = jnp.concatenate(
                [jnp.where(mask, pieces[v][part].astype(F32), 0.0) for v in range(4)], axis=0
            ).astype(BF16)
            packed = packed + dot_nt(onehot16, table)
    req_out[:, 0, :] = packed[:, 0:128]
    req_out[:, 1, :] = packed[:, 128:256]

    pl.semaphore_wait(barrier, DEV - 1)
    exchange(req_out, req_in, 0, False)
    req_in[0] = req_out[0]

    tab_copy.wait()
    for f in range(FIELDS):
        tabt[f * NODES : (f + 1) * NODES, :] = tab[f].T

    cos_p, sin_p = sincos_twice(angle_ref[...] * 0.5)
    axial = axial_ref[...]
    zero = jnp.zeros((5, PTS), F32)
    cols[...] = jnp.concatenate([cos_p, sin_p, axial, zero], axis=0).T
    cos_o, sin_o = sincos_twice(oang_ref[...] * 0.5)
    orad = orad_ref[...]
    obs_x = orad * cos_o
    obs_y = orad * sin_o
    obs_z = oax_ref[...]

    @pl.loop(0, PTS // 16)
    def _(step):
        rows = pl.ds(pl.multiple_of(step * 16, 16), 16)
        own = cols[rows, :]
        px = own[:, 0:1]
        py = own[:, 1:2]
        pz = own[:, 2:3]
        for g in range(2):
            lanes = slice(g * 128, (g + 1) * 128)
            dx = obs_x[:, lanes] - px
            dy = obs_y[:, lanes] - py
            dz = obs_z[:, lanes] - pz
            square = dx * dx + dy * dy + dz * dz
            inv = lax.rsqrt(square)
            dist = square * inv
            turns = jnp.round(dist * (0.125 / math.pi))
            r = dist * 0.125 - turns * PI_HI - turns * PI_LO
            c1, s1 = sincos_twice(r)
            t = c1 + c1
            c2 = t * c1 - 1.0
            s2 = t * s1
            c3 = t * c2 - c1
            s3 = t * s2 - s1
            c4 = t * c3 - c2
            s4 = t * s3 - s2
            c5 = t * c4 - c3
            s5 = t * s4 - s3
            t5 = c5 + c5
            c10 = t5 * c5 - 1.0
            s10 = t5 * s5
            c9 = t5 * c4 - c1
            t9 = c9 + c9
            c19 = t9 * c10 - c1
            s19 = t9 * s10 - s1
            c28 = t9 * c19 - c10
            s28 = t9 * s19 - s10
            inv_ref[rows, lanes] = inv
            for n, value in enumerate((c1, s1, c2, s2, c3, s3, c4, s4)):
                ys[n, rows, lanes] = value
            for n, value in enumerate((c10, s10, c19, s19, c28, s28)):
                xs[n, rows, lanes] = value

    whole(req_in, 0).wait_recv()

    first = req_in[:, 0, :].T
    second = req_in[:, 1, :].T
    rid[...] = first[0:CAP]
    for n, value in enumerate((first[CAP : 2 * CAP], second[0:CAP], second[CAP : 2 * CAP])):
        for i, weight in enumerate(lagrange(value)):
            lag[:, n * 8 + i, :] = weight

    elem_iota = lax.broadcasted_iota(jnp.int32, (ELEM, 128), 0).astype(F32)

    @pl.loop(0, CAP // 2)
    def _(pair):
        picks = []
        weights = []
        for half in range(2):
            c = pair * 2 + half
            picks.append(jnp.where(elem_iota == rid[pl.ds(c, 1), :], 1.0, 0.0).astype(BF16))
            weights.append(lag[c])
        pick = jnp.concatenate(picks, axis=1)
        weight = jnp.concatenate(weights, axis=1)
        for f in range(FIELDS):
            nodal = dot_nn(tabt[f * NODES : (f + 1) * NODES, :], pick)
            total = None
            for i in range(8):
                inner = None
                for j in range(8):
                    at = (i * 8 + j) * 8
                    term = nodal[at : at + 8, :] * weight[8 + j : 9 + j, :]
                    inner = term if inner is None else inner + term
                inner = inner * weight[i : i + 1, :]
                total = inner if total is None else total + inner
            value = jnp.sum(total * weight[16:24, :], axis=0, keepdims=True)
            valt[pl.ds(f * CAP + pair * 2, 1), :] = value[:, 0:128]
            valt[pl.ds(f * CAP + pair * 2 + 1, 1), :] = value[:, 128:256]

    valt[FIELDS * CAP : 384, :] = jnp.zeros((384 - FIELDS * CAP, 128), F32)
    for n in range(3):
        rep_out[:, n, :] = valt[n * 128 : (n + 1) * 128, :].T
    exchange(rep_out, rep_in, 1, False, back=True)
    rep_in[0] = rep_out[0]
    whole(rep_in, 1).wait_recv()

    parts = [split2(rep_in[:, n, :].T) for n in range(3)]
    table = jnp.concatenate(
        [
            jnp.concatenate([hi for hi, lo in parts], axis=0),
            jnp.concatenate([lo for hi, lo in parts], axis=0),
        ],
        axis=1,
    )
    for blk in range(PTS // BLK):
        at = slice(blk * BLK, (blk + 1) * BLK)
        candidates = dot_nn(table, hot[:, at])
        mask = rankm[:, at]
        for f in range(FIELDS):
            surf_ref[f : f + 1, at] = jnp.sum(
                candidates[f * CAP : (f + 1) * CAP, :] * mask, axis=0, keepdims=True
            )

    density = surf_ref[0:1, :]
    vel_x = surf_ref[1:2, :]
    vel_y = surf_ref[2:3, :]
    vel_z = surf_ref[3:4, :]
    pressure = surf_ref[4:5, :]
    normal = vel_x * cos_p + vel_y * sin_p
    scaled = weight_ref[...] * (1.0 / math.sqrt(PTS * DEV))
    flux = density * normal * scaled
    pressure = pressure * scaled
    coefs[...] = jnp.concatenate(
        [
            flux,
            pressure * cos_p + flux * vel_x,
            pressure * sin_p + flux * vel_y,
            flux * vel_z,
            -(pressure + flux * (normal + vel_z * axial)),
            jnp.zeros((3, PTS), F32),
        ],
        axis=0,
    ).T

    @pl.loop(0, PTS // 32)
    def _(step):
        rows = pl.ds(pl.multiple_of(step * 32, 32), 32)
        own = coefs[rows, :]
        for g in range(2):
            lanes = slice(g * 128, (g + 1) * 128)
            inv = inv_ref[rows, lanes]
            linear = (
                own[:, 1:2] * obs_x[:, lanes]
                + own[:, 2:3] * obs_y[:, lanes]
                + own[:, 3:4] * obs_z[:, lanes]
                + own[:, 4:5]
            )
            amp[rows, lanes] = (own[:, 0:1] + linear * inv) * (inv * orad[:, lanes])

    UNROLL = 8
    for g in range(2):
        lanes = slice(g * 128, (g + 1) * 128)
        for number, (centre, reach) in enumerate(CENTRES):

            def body(step, acc, number=number, reach=reach, lanes=lanes):
                acc = list(acc)
                for u in range(UNROLL):
                    rows = pl.ds(pl.multiple_of(step * (8 * UNROLL) + u * 8, 8), 8)
                    a = amp[rows, lanes]
                    if number == 0:
                        ac = a * ys[4, rows, lanes]
                        as_ = a * ys[5, rows, lanes]
                    else:
                        ac = a * xs[2 * number - 2, rows, lanes]
                        as_ = a * xs[2 * number - 1, rows, lanes]
                    acc[0] = acc[0] + ac
                    acc[1] = acc[1] + as_
                    for b in range(reach):
                        yc = ys[2 * b, rows, lanes]
                        ysn = ys[2 * b + 1, rows, lanes]
                        acc[2 + 4 * b] = acc[2 + 4 * b] + ac * yc
                        acc[3 + 4 * b] = acc[3 + 4 * b] + as_ * ysn
                        acc[4 + 4 * b] = acc[4 + 4 * b] + as_ * yc
                        acc[5 + 4 * b] = acc[5 + 4 * b] + ac * ysn
                return tuple(acc)

            start = tuple(jnp.zeros((8, 128), F32) for _ in range(2 + 4 * reach))
            acc = lax.fori_loop(0, PTS // (8 * UNROLL), body, start)

            def put(k, cosine, sine, lanes=lanes):
                sums[k - 1 : k, lanes] = jnp.sum(cosine, axis=0, keepdims=True)
                sums[NFREQ + k - 1 : NFREQ + k, lanes] = jnp.sum(sine, axis=0, keepdims=True)

            put(centre, acc[0], acc[1])
            for b in range(reach):
                p1, p2, p3, p4 = acc[2 + 4 * b : 6 + 4 * b]
                put(centre + b + 1, p1 - p2, p3 + p4)
                put(centre - b - 1, p1 + p2, p3 - p4)

    slot = slot_ref[...]
    col_iota = lax.broadcasted_iota(jnp.int32, (DEV, NOBS), 0) * 2
    pieces = split3(sums[...])
    placed = []
    for parity in range(2):
        choose = jnp.where(col_iota + parity == slot, 1.0, 0.0).astype(BF16)
        placed.append(dot_nt(choose, pieces[0]) + dot_nt(choose, pieces[1]) + dot_nt(choose, pieces[2]))
    red_out[:, 0, :] = jnp.concatenate(placed, axis=1)
    exchange(red_out, red_in, 2, True)
    red_in[0] = red_out[me]
    cos_f, sin_f = sincos_twice(phase_ref[...] * 0.5)
    whole(red_in, 2).wait_recv()
    total = jnp.sum(red_in[:, 0, :], axis=0, keepdims=True)
    for parity in range(2):
        cosine = total[:, parity * 64 : parity * 64 + 32]
        sine = total[:, parity * 64 + 32 : parity * 64 + 64]
        spec_ref[0, parity : parity + 1, :] = prior_ref[0, parity : parity + 1, :] + (
            cos_f * cosine - sin_f * sine
        )
        spec_ref[1, parity : parity + 1, :] = prior_ref[1, parity : parity + 1, :] - (
            sin_f * cosine + cos_f * sine
        )
    whole(req_in, 0).wait_send()
    whole(rep_in, 1).wait_send()
    whole(red_in, 2).wait_send()


def on_device(
    element_fields,
    ref_coords,
    local_element,
    owner,
    point_angle,
    point_axial,
    panel_weight,
    obs_radius,
    obs_angle,
    obs_axial,
    step_phase,
    observer_slot,
    prior_spectra,
):
    vmem = pl.BlockSpec(memory_space=pltpu.VMEM)
    surface, spectra = pl.pallas_call(
        kernel,
        out_shape=(
            jax.ShapeDtypeStruct((FIELDS, PTS), F32),
            jax.ShapeDtypeStruct((2, 2, NFREQ), F32),
        ),
        in_specs=[pl.BlockSpec(memory_space=pl.ANY)] + [vmem] * 12,
        out_specs=(vmem, vmem),
        scratch_shapes=[
            pltpu.VMEM((FIELDS, ELEM, NODES), BF16),
            pltpu.VMEM((FIELDS * NODES, ELEM), BF16),
            pltpu.VMEM((2 * DEV, PTS), BF16),
            pltpu.VMEM((CAP, PTS), F32),
            pltpu.VMEM((DEV, 2, 128), F32),
            pltpu.VMEM((DEV, 2, 128), F32),
            pltpu.VMEM((CAP, 128), F32),
            pltpu.VMEM((CAP, 24, 128), F32),
            pltpu.VMEM((384, 128), F32),
            pltpu.VMEM((DEV, 3, 128), F32),
            pltpu.VMEM((DEV, 3, 128), F32),
            pltpu.VMEM((PTS, 8), F32),
            pltpu.VMEM((PTS, 8), F32),
            pltpu.VMEM((PTS, NOBS), F32),
            pltpu.VMEM((PTS, NOBS), F32),
            pltpu.VMEM((8, PTS, NOBS), F32),
            pltpu.VMEM((6, PTS, NOBS), F32),
            pltpu.VMEM((2 * NFREQ, NOBS), F32),
            pltpu.VMEM((DEV, 1, 128), F32),
            pltpu.VMEM((DEV, 1, 128), F32),
            pltpu.SemaphoreType.DMA,
            pltpu.SemaphoreType.DMA((6,)),
        ],
        compiler_params=pltpu.CompilerParams(
            collective_id=0, has_side_effects=True, vmem_limit_bytes=63 * 1024 * 1024
        ),
        name="flow",
    )(
        element_fields.transpose(1, 0, 2),
        ref_coords,
        local_element.reshape(1, PTS),
        owner.reshape(1, PTS),
        point_angle.reshape(1, PTS),
        point_axial.reshape(1, PTS),
        panel_weight.reshape(1, PTS),
        obs_radius.reshape(1, NOBS),
        obs_angle.reshape(1, NOBS),
        obs_axial.reshape(1, NOBS),
        step_phase.reshape(1, NFREQ),
        observer_slot.reshape(1, NOBS),
        prior_spectra.transpose(0, 2, 1),
    )
    return surface, spectra.transpose(0, 2, 1)


def solution(mesh):
    return jax.shard_map(
        on_device,
        mesh=mesh,
        in_specs=(
            P(("gx", "gy"), None, None),
            P(None, ("gx", "gy")),
            P(("gx", "gy")),
            P(("gx", "gy"), None),
            P(("gx", "gy")),
            P(("gx", "gy")),
            P(("gx", "gy")),
            P(),
            P(),
            P(),
            P(),
            P(),
            P(None, None, ("gx", "gy")),
        ),
        out_specs=(P(None, ("gx", "gy")), P(None, None, ("gx", "gy"))),
        check_vma=False,
    )
```

time: 695 us -> 99.4 us (0.14)
  other arithmetic: 396 us -> 0 us
  local copies, waits for them, and re-layouts: 168 us -> 2.72 us
  Pallas kernels: 0 us -> 95.8 us
  waiting for transfers between devices: 82.7 us -> 0 us
  starting transfers between devices: 32.1 us -> 0 us
  between operations: 14.4 us -> 0.64 us
    reduce_sum x10 -> x0, other arithmetic: 253 us -> none  [the longest x8 249 us: spectra_terms(): cos_sum = jnp.sum(amplitude[:, :, None] * jnp.cos(phases), axis=0).T]
    while x8 -> x0, other arithmetic: 127 us -> none
    gather x9 -> x0, local copies, waits for them, and re-layouts: 104 us -> none  [the longest x8 96.1 us: sample(): gathered = jnp.take(fields, pieces[0], axis=0).astype(jnp.float32)]
    pallas_call x0 -> x1, Pallas kernels: none -> 95.8 us  [on_device(): pl.pallas_call(kernel, out_shape=(jax.ShapeDtypeStruct((FIELDS, PTS), F32...]
    all_gather x1 -> x0, waiting for transfers between devices: 65.4 us -> none  [total_of_pieces(): tiles = lax.all_gather(value, axis)]
    all_to_all x5 -> x0, starting transfers between devices: 31.8 us -> none  [the longest x1 9.42 us: on_device(): lax.all_to_all(send_ids.reshape(1, outer, inner, capacity), 'gy', split_a...]
    scatter x4 -> x0, local copies, waits for them, and re-layouts: 24.1 us -> none  [the longest x1 8.25 us: on_device(): jnp.zeros((devices * capacity,), jnp.int32).at[position].set(local_element)]
    while x26 -> x0, local copies, waits for them, and re-layouts: 18.6 us -> none
  transfers between devices with their start and end apart: 6 -> 0, of which waited for: 4 -> 0; matrix products, arithmetic and copies ran while one was open for 3% -> 0% of each run, Pallas kernels for 0% -> 0%
where the time goes in v1:
time: 99.4 us; the launch traced here: 99.2 us
  Pallas kernels  95.8 us (96%)
  local copies, waits for them, and re-layouts  2.72 us (3%)
    pallas_call x1, Pallas kernels, on_device(): pl.pallas_call(kernel, out_shape=(jax.ShapeDtypeStruct((FIELDS, PTS), F32...  95.8 us
    unnamed x2, local copies, waits for them, and re-layouts  2.72 us

profile of v1, /device:TPU:1, one launch (start us, length us, event | category | flops | bytes accessed | tf_op | source)
XLA Modules:
  0.0 99.2 jit_solution(13196116874854532147)
XLA Ops:
  0.6 95.8 %flow.1 = (f32[5,2048]{1,0:T(8,128)}, f32[2,2,32]{2,1,0:T(2,128)}) custom-call(bf16[5,512,512]{2,1,0:T(8,128)(2,1)} %bitcast.13, f32[3,2048]{1,0:T(4,128)} %coords_ref.1, s32[1,2048]{1,0:T(1,128)} %bitcast.14, s32[1,2048]{1,0:T(1,128)} %bitcast.15, f32[1,2048]{1,0:T(1,128)} %bitcast.16, f32[1,2048]{1,0:T(1,128)} %bitcast.17, f32[1,2048]{1,0:T(1,128)} %bitcast.18, ...), custom_call_target="tpu_custom_call" | custom-call | tf_op jit(solution)/shard_map/flow/pallas_call | solution.py:470
  96.5 1.5 %copy.17 = f32[5,2048]{1,0:T(8,128)} copy(f32[5,2048]{1,0:T(8,128)} %get-tuple-element.8) | data formatting | bytes 81920
  98.0 1.2 %copy.18 = f32[2,32,2]{1,2,0:T(2,128)} copy(f32[2,32,2]{1,2,0:T(2,128)} %bitcast.20) | data formatting | bytes 1024

commit v2 on v1

--- a/solution.py
+++ b/solution.py
@@ -8,7 +8,7 @@
 from jax.experimental.pallas import tpu as pltpu
 from jax.sharding import PartitionSpec as P
 
-MESH = pl.DeviceIdType.MESH
+LOGICAL = pl.DeviceIdType.LOGICAL
 F32 = jnp.float32
 BF16 = jnp.bfloat16
 
@@ -22,6 +22,7 @@
 NOBS = 256
 NFREQ = 32
 BLK = 256
+WIDE = 4
 
 GLL = [
     -1.0,
@@ -107,6 +108,15 @@
     mid = rest.astype(BF16)
     lo = (rest - mid.astype(F32)).astype(BF16)
     return hi, mid, lo
+
+
+def products(left, right, mine, theirs):
+    a = [piece.astype(F32) for piece in split3(mine)]
+    b = [piece.astype(F32) for piece in split3(theirs)]
+    for i in range(3):
+        for j in range(3 - i):
+            left.append(a[i])
+            right.append(b[j])
 
 
 def dot_nt(a, b):
@@ -144,12 +154,9 @@
     valt,
     rep_out,
     rep_in,
-    cols,
-    coefs,
+    square_ref,
     amp,
-    inv_ref,
-    ys,
-    xs,
+    geo,
     sums,
     red_out,
     red_in,
@@ -159,41 +166,44 @@
     me = lax.axis_index("gx") * INNER + lax.axis_index("gy")
 
     def target(d):
-        flat = lax.rem(me + d, DEV)
-        return flat, (flat // INNER, lax.rem(flat, INNER))
+        return lax.rem(me + d, DEV)
+
+    def others(body):
+        @pl.loop(0, 18)
+        def _(step):
+            for u in range(7):
+                body(step * 7 + (u + 1))
+
+        body(DEV - 1)
 
     tab_copy = pltpu.make_async_copy(tab_hbm, tab, tab_sem)
     tab_copy.start()
     barrier = pltpu.get_barrier_semaphore()
-
-    @pl.loop(1, DEV)
-    def _(d):
-        flat, where = target(d)
-        pl.semaphore_signal(barrier, inc=1, device_id=where, device_id_type=MESH)
+    others(lambda d: pl.semaphore_signal(barrier, inc=1, device_id=target(d), device_id_type=LOGICAL))
 
     def exchange(source, landing, k, own, back=False):
-        @pl.loop(1, DEV)
-        def _(d):
-            flat, where = target(DEV - d if back else d)
+        def send(d):
+            flat = target(DEV - d if back else d)
             pltpu.make_async_remote_copy(
                 src_ref=source.at[flat if own else d],
                 dst_ref=landing.at[d],
                 send_sem=sems.at[2 * k],
                 recv_sem=sems.at[2 * k + 1],
-                device_id=where,
-                device_id_type=MESH,
+                device_id=flat,
+                device_id_type=LOGICAL,
             ).start()
+
+        others(send)
 
     def whole(landing, k):
         rest = landing.at[pl.ds(1, DEV - 1)]
-        flat, where = target(1)
         return pltpu.make_async_remote_copy(
             src_ref=rest,
             dst_ref=rest,
             send_sem=sems.at[2 * k],
             recv_sem=sems.at[2 * k + 1],
-            device_id=where,
-            device_id_type=MESH,
+            device_id=target(1),
+            device_id_type=LOGICAL,
         )
 
     rel = owner_ref[...] - me
@@ -228,65 +238,71 @@
     req_out[:, 0, :] = packed[:, 0:128]
     req_out[:, 1, :] = packed[:, 128:256]
 
-    pl.semaphore_wait(barrier, DEV - 1)
-    exchange(req_out, req_in, 0, False)
-    req_in[0] = req_out[0]
-
-    tab_copy.wait()
-    for f in range(FIELDS):
-        tabt[f * NODES : (f + 1) * NODES, :] = tab[f].T
-
     cos_p, sin_p = sincos_twice(angle_ref[...] * 0.5)
     axial = axial_ref[...]
-    zero = jnp.zeros((5, PTS), F32)
-    cols[...] = jnp.concatenate([cos_p, sin_p, axial, zero], axis=0).T
     cos_o, sin_o = sincos_twice(oang_ref[...] * 0.5)
     orad = orad_ref[...]
     obs_x = orad * cos_o
     obs_y = orad * sin_o
     obs_z = oax_ref[...]
-
-    @pl.loop(0, PTS // 16)
-    def _(step):
-        rows = pl.ds(pl.multiple_of(step * 16, 16), 16)
-        own = cols[rows, :]
-        px = own[:, 0:1]
-        py = own[:, 1:2]
-        pz = own[:, 2:3]
-        for g in range(2):
-            lanes = slice(g * 128, (g + 1) * 128)
-            dx = obs_x[:, lanes] - px
-            dy = obs_y[:, lanes] - py
-            dz = obs_z[:, lanes] - pz
-            square = dx * dx + dy * dy + dz * dz
-            inv = lax.rsqrt(square)
-            dist = square * inv
-            turns = jnp.round(dist * (0.125 / math.pi))
-            r = dist * 0.125 - turns * PI_HI - turns * PI_LO
-            c1, s1 = sincos_twice(r)
-            t = c1 + c1
-            c2 = t * c1 - 1.0
-            s2 = t * s1
-            c3 = t * c2 - c1
-            s3 = t * s2 - s1
-            c4 = t * c3 - c2
-            s4 = t * s3 - s2
-            c5 = t * c4 - c3
-            s5 = t * s4 - s3
-            t5 = c5 + c5
-            c10 = t5 * c5 - 1.0
-            s10 = t5 * s5
-            c9 = t5 * c4 - c1
-            t9 = c9 + c9
-            c19 = t9 * c10 - c1
-            s19 = t9 * s10 - s1
-            c28 = t9 * c19 - c10
-            s28 = t9 * s19 - s10
-            inv_ref[rows, lanes] = inv
-            for n, value in enumerate((c1, s1, c2, s2, c3, s3, c4, s4)):
-                ys[n, rows, lanes] = value
-            for n, value in enumerate((c10, s10, c19, s19, c28, s28)):
-                xs[n, rows, lanes] = value
+    mid_p = axial - 4.0
+    mid_o = obs_z - 4.0
+    left, right = [], []
+    for mine, theirs in ((cos_p * -2.0, obs_x), (sin_p * -2.0, obs_y), (mid_p * -2.0, mid_o)):
+        products(left, right, mine, theirs)
+    one_p = jnp.ones((1, PTS), F32)
+    one_o = jnp.ones((1, NOBS), F32)
+    for piece in split3(mid_p * mid_p + 1.0):
+        left.append(piece.astype(F32))
+        right.append(one_o)
+    for piece in split3(orad * orad + mid_o * mid_o):
+        left.append(one_p)
+        right.append(piece.astype(F32))
+    square_ref[...] = dot_nn(jnp.concatenate(left, axis=0).T.astype(BF16), jnp.concatenate(right, axis=0).astype(BF16))
+    tab_copy.wait()
+    for f in range(FIELDS):
+        tabt[f * NODES : (f + 1) * NODES, :] = tab[f].T
+
+    pl.semaphore_wait(barrier, DEV - 1)
+    exchange(req_out, req_in, 0, False)
+    req_in[0] = req_out[0]
+
+    def geometry(first, last):
+        @pl.loop(first, last)
+        def _(step):
+            for u in range(2):
+                blk = step * 2 + u
+                for g in range(2):
+                    square = square_ref[pl.ds(pl.multiple_of(blk * 8, 8), 8), g * 128 : (g + 1) * 128]
+                    inv = lax.rsqrt(square)
+                    dist = square * inv
+                    turns = jnp.round(dist * (0.125 / math.pi))
+                    r = dist * 0.125 - turns * PI_HI - turns * PI_LO
+                    c1, s1 = sincos_twice(r)
+                    t = c1 + c1
+                    c2 = t * c1 - 1.0
+                    s2 = t * s1
+                    c3 = t * c2 - c1
+                    s3 = t * s2 - s1
+                    c4 = t * c3 - c2
+                    s4 = t * s3 - s2
+                    c5 = t * c4 - c3
+                    s5 = t * s4 - s3
+                    t5 = c5 + c5
+                    c10 = t5 * c5 - 1.0
+                    s10 = t5 * s5
+                    c9 = t5 * c4 - c1
+                    t9 = c9 + c9
+                    c19 = t9 * c10 - c1
+                    s19 = t9 * s10 - s1
+                    c28 = t9 * c19 - c10
+                    s28 = t9 * s19 - s10
+                    for n, value in enumerate(
+                        (c1, s1, c2, s2, c3, s3, c4, s4, c10, s10, c19, s19, c28, s28, inv)
+                    ):
+                        geo[blk, g, n] = value
+
+    geometry(0, 52)
 
     whole(req_in, 0).wait_recv()
 
@@ -299,12 +315,12 @@
 
     elem_iota = lax.broadcasted_iota(jnp.int32, (ELEM, 128), 0).astype(F32)
 
-    @pl.loop(0, CAP // 2)
-    def _(pair):
+    @pl.loop(0, CAP // WIDE)
+    def _(group):
         picks = []
         weights = []
-        for half in range(2):
-            c = pair * 2 + half
+        for part in range(WIDE):
+            c = group * WIDE + part
             picks.append(jnp.where(elem_iota == rid[pl.ds(c, 1), :], 1.0, 0.0).astype(BF16))
             weights.append(lag[c])
         pick = jnp.concatenate(picks, axis=1)
@@ -321,14 +337,15 @@
                 inner = inner * weight[i : i + 1, :]
                 total = inner if total is None else total + inner
             value = jnp.sum(total * weight[16:24, :], axis=0, keepdims=True)
-            valt[pl.ds(f * CAP + pair * 2, 1), :] = value[:, 0:128]
-            valt[pl.ds(f * CAP + pair * 2 + 1, 1), :] = value[:, 128:256]
+            for part in range(WIDE):
+                valt[pl.ds(f * CAP + group * WIDE + part, 1), :] = value[:, part * 128 : (part + 1) * 128]
 
     valt[FIELDS * CAP : 384, :] = jnp.zeros((384 - FIELDS * CAP, 128), F32)
     for n in range(3):
         rep_out[:, n, :] = valt[n * 128 : (n + 1) * 128, :].T
     exchange(rep_out, rep_in, 1, False, back=True)
     rep_in[0] = rep_out[0]
+    geometry(52, PTS // 16)
     whole(rep_in, 1).wait_recv()
 
     parts = [split2(rep_in[:, n, :].T) for n in range(3)]
@@ -357,54 +374,53 @@
     scaled = weight_ref[...] * (1.0 / math.sqrt(PTS * DEV))
     flux = density * normal * scaled
     pressure = pressure * scaled
-    coefs[...] = jnp.concatenate(
-        [
-            flux,
-            pressure * cos_p + flux * vel_x,
-            pressure * sin_p + flux * vel_y,
-            flux * vel_z,
-            -(pressure + flux * (normal + vel_z * axial)),
-            jnp.zeros((3, PTS), F32),
-        ],
-        axis=0,
-    ).T
-
-    @pl.loop(0, PTS // 32)
-    def _(step):
-        rows = pl.ds(pl.multiple_of(step * 32, 32), 32)
-        own = coefs[rows, :]
-        for g in range(2):
-            lanes = slice(g * 128, (g + 1) * 128)
-            inv = inv_ref[rows, lanes]
-            linear = (
-                own[:, 1:2] * obs_x[:, lanes]
-                + own[:, 2:3] * obs_y[:, lanes]
-                + own[:, 3:4] * obs_z[:, lanes]
-                + own[:, 4:5]
-            )
-            amp[rows, lanes] = (own[:, 0:1] + linear * inv) * (inv * orad[:, lanes])
+    left, right = [], []
+    products(left, right, pressure * cos_p + flux * vel_x, obs_x)
+    products(left, right, pressure * sin_p + flux * vel_y, obs_y)
+    products(left, right, flux * vel_z, obs_z)
+    for piece in split3(-(pressure + flux * (normal + vel_z * axial))):
+        left.append(piece.astype(F32))
+        right.append(one_o)
+    zero_o = jnp.zeros((1, NOBS), F32)
+    other = [zero_o] * len(left)
+    for piece in split3(flux):
+        left.append(piece.astype(F32))
+        right.append(zero_o)
+        other.append(one_o)
+    left = jnp.concatenate(left, axis=0).T.astype(BF16)
+    right = jnp.concatenate(
+        [jnp.concatenate(right, axis=0), jnp.concatenate(other, axis=0)], axis=1
+    ).astype(BF16)
+    for blk in range(PTS // BLK):
+        mixed = dot_nn(left[blk * BLK : (blk + 1) * BLK, :], right)
+        for n in range(BLK // 8):
+            at = blk * (BLK // 8) + n
+            for g in range(2):
+                lanes = slice(g * 128, (g + 1) * 128)
+                inv = geo[at, g, 14]
+                linear = mixed[n * 8 : n * 8 + 8, lanes]
+                amp[at, g] = (mixed[n * 8 : n * 8 + 8, 256 + g * 128 : 384 + g * 128] + linear * inv) * (
+                    inv * orad[:, lanes]
+                )
 
     UNROLL = 8
     for g in range(2):
         lanes = slice(g * 128, (g + 1) * 128)
         for number, (centre, reach) in enumerate(CENTRES):
 
-            def body(step, acc, number=number, reach=reach, lanes=lanes):
+            def body(step, acc, number=number, reach=reach, g=g):
                 acc = list(acc)
                 for u in range(UNROLL):
-                    rows = pl.ds(pl.multiple_of(step * (8 * UNROLL) + u * 8, 8), 8)
-                    a = amp[rows, lanes]
-                    if number == 0:
-                        ac = a * ys[4, rows, lanes]
-                        as_ = a * ys[5, rows, lanes]
-                    else:
-                        ac = a * xs[2 * number - 2, rows, lanes]
-                        as_ = a * xs[2 * number - 1, rows, lanes]
+                    blk = step * UNROLL + u
+                    a = amp[blk, g]
+                    at = 4 if number == 0 else 6 + 2 * number
+                    ac = a * geo[blk, g, at]
+                    as_ = a * geo[blk, g, at + 1]
                     acc[0] = acc[0] + ac
                     acc[1] = acc[1] + as_
                     for b in range(reach):
-                        yc = ys[2 * b, rows, lanes]
-                        ysn = ys[2 * b + 1, rows, lanes]
+                        yc = geo[blk, g, 2 * b]
+                        ysn = geo[blk, g, 2 * b + 1]
                         acc[2 + 4 * b] = acc[2 + 4 * b] + ac * yc
                         acc[3 + 4 * b] = acc[3 + 4 * b] + as_ * ysn
                         acc[4 + 4 * b] = acc[4 + 4 * b] + as_ * yc
@@ -487,12 +503,9 @@
             pltpu.VMEM((384, 128), F32),
             pltpu.VMEM((DEV, 3, 128), F32),
             pltpu.VMEM((DEV, 3, 128), F32),
-            pltpu.VMEM((PTS, 8), F32),
-            pltpu.VMEM((PTS, 8), F32),
             pltpu.VMEM((PTS, NOBS), F32),
-            pltpu.VMEM((PTS, NOBS), F32),
-            pltpu.VMEM((8, PTS, NOBS), F32),
-            pltpu.VMEM((6, PTS, NOBS), F32),
+            pltpu.VMEM((PTS // 8, 2, 8, 128), F32),
+            pltpu.VMEM((PTS // 8, 2, 15, 8, 128), F32),
             pltpu.VMEM((2 * NFREQ, NOBS), F32),
             pltpu.VMEM((DEV, 1, 128), F32),
             pltpu.VMEM((DEV, 1, 128), F32),

time: 99.4 us -> 72.4 us (0.73)
  Pallas kernels: 95.8 us -> 68.8 us
    pallas_call x1, Pallas kernels: 95.8 us -> 68.8 us  [on_device(): pl.pallas_call(kernel, out_shape=(jax.ShapeDtypeStruct((FIELDS, PTS), F32...]
where the time goes in v2:
time: 72.4 us; the launch traced here: 72.2 us
  Pallas kernels  68.8 us (95%)
  local copies, waits for them, and re-layouts  2.72 us (4%)
    pallas_call x1, Pallas kernels, on_device(): pl.pallas_call(kernel, out_shape=(jax.ShapeDtypeStruct((FIELDS, PTS), F32...  68.8 us
    unnamed x2, local copies, waits for them, and re-layouts  2.72 us

profile of v2, /device:TPU:1, one launch (start us, length us, event | category | flops | bytes accessed | tf_op | source)
XLA Modules:
  0.0 72.2 jit_solution(15702624962015452420)
XLA Ops:
  0.6 68.8 %flow.1 = (f32[5,2048]{1,0:T(8,128)}, f32[2,2,32]{2,1,0:T(2,128)}) custom-call(bf16[5,512,512]{2,1,0:T(8,128)(2,1)} %bitcast.13, f32[3,2048]{1,0:T(4,128)} %coords_ref.1, s32[1,2048]{1,0:T(1,128)} %bitcast.14, s32[1,2048]{1,0:T(1,128)} %bitcast.15, f32[1,2048]{1,0:T(1,128)} %bitcast.16, f32[1,2048]{1,0:T(1,128)} %bitcast.17, f32[1,2048]{1,0:T(1,128)} %bitcast.18, ...), custom_call_target="tpu_custom_call" | custom-call | tf_op jit(solution)/shard_map/flow/pallas_call | solution.py:486
  69.5 1.5 %copy.17 = f32[5,2048]{1,0:T(8,128)} copy(f32[5,2048]{1,0:T(8,128)} %get-tuple-element.8) | data formatting | bytes 81920
  70.9 1.2 %copy.18 = f32[2,32,2]{1,2,0:T(2,128)} copy(f32[2,32,2]{1,2,0:T(2,128)} %bitcast.20) | data formatting | bytes 1024

commit v3 on v2

--- a/solution.py
+++ b/solution.py
@@ -22,7 +22,14 @@
 NOBS = 256
 NFREQ = 32
 BLK = 256
-WIDE = 4
+WIDE = 8
+UNROLL = 16
+SOON = 48
+SOON_PTS = PTS * SOON // CAP
+DELTAS = sorted(
+    [(a, b, c, d) for a in range(4) for b in range(4) for c in range(4) for d in range(2)][1:],
+    key=lambda t: -sum(min(v, 4 - v) for v in t[:3]) - 0.3 * t[3],
+)
 
 GLL = [
     -1.0,
@@ -152,8 +159,15 @@
     rid,
     lag,
     valt,
+    valt_b,
     rep_out,
     rep_in,
+    rep_out_b,
+    rep_in_b,
+    swap,
+    hot_p,
+    rankm_p,
+    partial,
     square_ref,
     amp,
     geo,
@@ -165,31 +179,36 @@
 ):
     me = lax.axis_index("gx") * INNER + lax.axis_index("gy")
 
-    def target(d):
-        return lax.rem(me + d, DEV)
+    y, x, z, core = me // 32, lax.rem(me // 8, 4), lax.rem(me // 2, 4), lax.rem(me, 2)
+
+    def target(delta):
+        dy, dx, dz, dc = delta
+        return (
+            lax.rem(y + dy, 4) * 32 + lax.rem(x + dx, 4) * 8 + lax.rem(z + dz, 4) * 2 + lax.rem(core + dc, 2)
+        )
 
     def others(body):
-        @pl.loop(0, 18)
-        def _(step):
-            for u in range(7):
-                body(step * 7 + (u + 1))
-
-        body(DEV - 1)
+        for delta in DELTAS:
+            code = delta[0] * 32 + delta[1] * 8 + delta[2] * 2 + delta[3]
+            body(code, target(delta), target(((4 - delta[0]) % 4, (4 - delta[1]) % 4, (4 - delta[2]) % 4, delta[3])))
 
     tab_copy = pltpu.make_async_copy(tab_hbm, tab, tab_sem)
     tab_copy.start()
     barrier = pltpu.get_barrier_semaphore()
-    others(lambda d: pl.semaphore_signal(barrier, inc=1, device_id=target(d), device_id_type=LOGICAL))
-
-    def exchange(source, landing, k, own, back=False):
-        def send(d):
-            flat = target(DEV - d if back else d)
+    others(
+        lambda code, there, back: pl.semaphore_signal(
+            barrier, inc=1, device_id=there, device_id_type=LOGICAL
+        )
+    )
+
+    def exchange(source, landing, k, own=False, reply=False):
+        def send(code, there, back):
             pltpu.make_async_remote_copy(
-                src_ref=source.at[flat if own else d],
-                dst_ref=landing.at[d],
+                src_ref=source.at[there if own else code],
+                dst_ref=landing.at[code],
                 send_sem=sems.at[2 * k],
                 recv_sem=sems.at[2 * k + 1],
-                device_id=flat,
+                device_id=back if reply else there,
                 device_id_type=LOGICAL,
             ).start()
 
@@ -202,12 +221,17 @@
             dst_ref=rest,
             send_sem=sems.at[2 * k],
             recv_sem=sems.at[2 * k + 1],
-            device_id=target(1),
+            device_id=lax.rem(me + 1, DEV),
             device_id_type=LOGICAL,
         )
 
-    rel = owner_ref[...] - me
-    rel = jnp.where(rel < 0, rel + DEV, rel)
+    own = owner_ref[...]
+    rel = (
+        ((own // 32 - y + 4) & 3) * 32
+        + (((own // 8) & 3) - x + 4 & 3) * 8
+        + (((own // 2) & 3) - z + 4 & 3) * 2
+        + ((own & 1) - core + 2 & 1)
+    )
     dev_iota = lax.broadcasted_iota(jnp.int32, (DEV, BLK), 0)
     cap_iota = lax.broadcasted_iota(jnp.int32, (CAP, BLK), 0)
     before = jnp.where(
@@ -217,6 +241,10 @@
     ).astype(BF16)
     offset = jnp.zeros((DEV, 1), F32)
     packed = jnp.zeros((DEV, 4 * CAP), F32)
+    swap_iota = lax.broadcasted_iota(jnp.int32, (PTS - SOON_PTS, BLK), 0)
+    count = jnp.zeros((1, 1), F32)
+    wrong = None
+    ranks, swaps = [], []
     for blk in range(PTS // BLK):
         at = slice(blk * BLK, (blk + 1) * BLK)
         onehot = jnp.where(dev_iota == rel[:, at], 1.0, 0.0)
@@ -226,6 +254,18 @@
         within = dot_nn(onehot16, before)
         rank = jnp.sum(onehot * (within + offset), axis=0, keepdims=True)
         offset = offset + jnp.sum(onehot, axis=1, keepdims=True)
+        if blk * BLK == SOON_PTS:
+            wrong = count
+            count = jnp.zeros((1, 1), F32)
+        flag = jnp.where(rank >= SOON if blk * BLK < SOON_PTS else rank < SOON, 1.0, 0.0)
+        number = dot_nn(jnp.broadcast_to(flag, (8, BLK)).astype(BF16), before)[0:1] + count
+        count = count + jnp.sum(flag, axis=1, keepdims=True)
+        if wrong is not None:
+            flag = jnp.where(number < wrong, flag, 0.0)
+        number = jnp.where(flag > 0.5, number, -1.0).astype(jnp.int32)
+        swap[:, at] = jnp.where(swap_iota == number, 1.0, 0.0).astype(BF16)
+        ranks.append(rank)
+        swaps.append(flag)
         mask = cap_iota == rank.astype(jnp.int32)
         rankm[:, at] = jnp.where(mask, 1.0, 0.0)
         rows = [local_ref[:, at].astype(F32)] + [coords_ref[v : v + 1, at] for v in range(3)]
@@ -239,7 +279,33 @@
     req_out[:, 1, :] = packed[:, 128:256]
 
     cos_p, sin_p = sincos_twice(angle_ref[...] * 0.5)
-    axial = axial_ref[...]
+    attributes = [piece.astype(F32) for row in (cos_p, sin_p, axial_ref[...], weight_ref[...]) for piece in split3(row)]
+    attributes.append(rel.astype(F32))
+    attributes.append(jnp.concatenate(ranks, axis=1))
+    attributes.append(jnp.zeros((2, PTS), F32))
+    attributes = jnp.concatenate(attributes, axis=0).astype(BF16)
+    to_first = dot_nt(attributes[:, SOON_PTS:], swap[:, SOON_PTS:]).astype(BF16)
+    to_last = dot_nt(attributes[:, :SOON_PTS], swap[:, :SOON_PTS]).astype(BF16)
+    moved = jnp.concatenate(
+        [dot_nn(to_first, swap[:, :SOON_PTS]), dot_nn(to_last, swap[:, SOON_PTS:])], axis=1
+    )
+    ordered = jnp.where(jnp.concatenate(swaps, axis=1) > 0.5, moved, attributes.astype(F32))
+    cos_p, sin_p, axial, panel = [
+        ordered[n : n + 1] + ordered[n + 1 : n + 2] + ordered[n + 2 : n + 3] for n in (0, 3, 6, 9)
+    ]
+    rel_p = ordered[12:13].astype(jnp.int32)
+    rank_p = ordered[13:14].astype(jnp.int32)
+    for blk in range(PTS // BLK):
+        at = slice(blk * BLK, (blk + 1) * BLK)
+        onehot16 = jnp.where(dev_iota == rel_p[:, at], 1.0, 0.0).astype(BF16)
+        hot_p[0:DEV, at] = onehot16
+        hot_p[DEV : 2 * DEV, at] = onehot16
+        rankm_p[:, at] = jnp.where(cap_iota == rank_p[:, at], 1.0, 0.0)
+
+    pl.semaphore_wait(barrier, DEV - 1)
+    exchange(req_out, req_in, 0)
+    req_in[0] = req_out[0]
+
     cos_o, sin_o = sincos_twice(oang_ref[...] * 0.5)
     orad = orad_ref[...]
     obs_x = orad * cos_o
@@ -262,10 +328,6 @@
     tab_copy.wait()
     for f in range(FIELDS):
         tabt[f * NODES : (f + 1) * NODES, :] = tab[f].T
-
-    pl.semaphore_wait(barrier, DEV - 1)
-    exchange(req_out, req_in, 0, False)
-    req_in[0] = req_out[0]
 
     def geometry(first, last):
         @pl.loop(first, last)
@@ -302,7 +364,7 @@
                     ):
                         geo[blk, g, n] = value
 
-    geometry(0, 52)
+    geometry(0, PTS // 16)
 
     whole(req_in, 0).wait_recv()
 
@@ -315,8 +377,7 @@
 
     elem_iota = lax.broadcasted_iota(jnp.int32, (ELEM, 128), 0).astype(F32)
 
-    @pl.loop(0, CAP // WIDE)
-    def _(group):
+    def gather(group, land, first, span):
         picks = []
         weights = []
         for part in range(WIDE):
@@ -338,107 +399,146 @@
                 total = inner if total is None else total + inner
             value = jnp.sum(total * weight[16:24, :], axis=0, keepdims=True)
             for part in range(WIDE):
-                valt[pl.ds(f * CAP + group * WIDE + part, 1), :] = value[:, part * 128 : (part + 1) * 128]
-
-    valt[FIELDS * CAP : 384, :] = jnp.zeros((384 - FIELDS * CAP, 128), F32)
-    for n in range(3):
+                land[pl.ds(f * span + (group * WIDE - first) + part, 1), :] = value[:, part * 128 : (part + 1) * 128]
+
+    pl.loop(0, SOON // WIDE)(lambda group: gather(group, valt, 0, SOON))
+    valt[FIELDS * SOON : 256, :] = jnp.zeros((256 - FIELDS * SOON, 128), F32)
+    for n in range(2):
         rep_out[:, n, :] = valt[n * 128 : (n + 1) * 128, :].T
-    exchange(rep_out, rep_in, 1, False, back=True)
+    exchange(rep_out, rep_in, 1, reply=True)
     rep_in[0] = rep_out[0]
-    geometry(52, PTS // 16)
+    pl.loop(SOON // WIDE, CAP // WIDE)(lambda group: gather(group, valt_b, SOON, CAP - SOON))
+    valt_b[FIELDS * (CAP - SOON) : 128, :] = jnp.zeros((128 - FIELDS * (CAP - SOON), 128), F32)
+    rep_out_b[:, 0, :] = valt_b[...].T
+    exchange(rep_out_b, rep_in_b, 3, reply=True)
+    rep_in_b[0] = rep_out_b[0]
+
+    def sources(landing, count):
+        parts = [split2(landing[:, n, :].T) for n in range(count)]
+        return jnp.concatenate(
+            [
+                jnp.concatenate([hi for hi, lo in parts], axis=0),
+                jnp.concatenate([lo for hi, lo in parts], axis=0),
+            ],
+            axis=1,
+        )
+
+    def pick(table, choose, mask, span):
+        found = dot_nn(table, choose)
+        return [
+            jnp.sum(found[f * span : (f + 1) * span, :] * mask, axis=0, keepdims=True) for f in range(FIELDS)
+        ]
+
+    def amplitudes(first, last, values):
+        at_p = slice(first * BLK, last * BLK)
+        density, vel_x, vel_y, vel_z, pressure = values
+        cos_q, sin_q, axial_q = cos_p[:, at_p], sin_p[:, at_p], axial[:, at_p]
+        normal = vel_x * cos_q + vel_y * sin_q
+        scaled = panel[:, at_p] * (1.0 / math.sqrt(PTS * DEV))
+        flux = density * normal * scaled
+        pressure = pressure * scaled
+        left, right = [], []
+        products(left, right, pressure * cos_q + flux * vel_x, obs_x)
+        products(left, right, pressure * sin_q + flux * vel_y, obs_y)
+        products(left, right, flux * vel_z, obs_z)
+        for piece in split3(-(pressure + flux * (normal + vel_z * axial_q))):
+            left.append(piece.astype(F32))
+            right.append(one_o)
+        zero_o = jnp.zeros((1, NOBS), F32)
+        other = [zero_o] * len(left)
+        for piece in split3(flux):
+            left.append(piece.astype(F32))
+            right.append(zero_o)
+            other.append(one_o)
+        left = jnp.concatenate(left, axis=0).T.astype(BF16)
+        right = jnp.concatenate(
+            [jnp.concatenate(right, axis=0), jnp.concatenate(other, axis=0)], axis=1
+        ).astype(BF16)
+        for blk in range(last - first):
+            mixed = dot_nn(left[blk * BLK : (blk + 1) * BLK, :], right)
+            for n in range(BLK // 8):
+                at = (first + blk) * (BLK // 8) + n
+                for g in range(2):
+                    lanes = slice(g * 128, (g + 1) * 128)
+                    inv = geo[at, g, 14]
+                    linear = mixed[n * 8 : n * 8 + 8, lanes]
+                    amp[at, g] = (
+                        mixed[n * 8 : n * 8 + 8, 256 + g * 128 : 384 + g * 128] + linear * inv
+                    ) * (inv * orad[:, lanes])
+
+    def put(k, lanes, cosine, sine):
+        sums[k - 1 : k, lanes] = jnp.sum(cosine, axis=0, keepdims=True)
+        sums[NFREQ + k - 1 : NFREQ + k, lanes] = jnp.sum(sine, axis=0, keepdims=True)
+
+    def green(first, last, begin, end):
+        for g in range(2):
+            lanes = slice(g * 128, (g + 1) * 128)
+            base = 0
+            for number, (centre, reach) in enumerate(CENTRES):
+
+                def body(step, acc, number=number, reach=reach, g=g):
+                    acc = list(acc)
+                    for u in range(UNROLL):
+                        blk = step * UNROLL + u
+                        a = amp[blk, g]
+                        at = 4 if number == 0 else 6 + 2 * number
+                        ac = a * geo[blk, g, at]
+                        as_ = a * geo[blk, g, at + 1]
+                        acc[0] = acc[0] + ac
+                        acc[1] = acc[1] + as_
+                        for b in range(reach):
+                            yc = geo[blk, g, 2 * b]
+                            ysn = geo[blk, g, 2 * b + 1]
+                            acc[2 + 4 * b] = acc[2 + 4 * b] + ac * yc
+                            acc[3 + 4 * b] = acc[3 + 4 * b] + as_ * ysn
+                            acc[4 + 4 * b] = acc[4 + 4 * b] + as_ * yc
+                            acc[5 + 4 * b] = acc[5 + 4 * b] + ac * ysn
+                    return tuple(acc)
+
+                count = 2 + 4 * reach
+                if begin:
+                    start = tuple(jnp.zeros((8, 128), F32) for _ in range(count))
+                else:
+                    start = tuple(partial[g, base + n] for n in range(count))
+                acc = lax.fori_loop(first // (8 * UNROLL), last // (8 * UNROLL), body, start)
+                if end:
+                    put(centre, lanes, acc[0], acc[1])
+                    for b in range(reach):
+                        p1, p2, p3, p4 = acc[2 + 4 * b : 6 + 4 * b]
+                        put(centre + b + 1, lanes, p1 - p2, p3 + p4)
+                        put(centre - b - 1, lanes, p1 + p2, p3 - p4)
+                else:
+                    for n in range(count):
+                        partial[g, base + n] = acc[n]
+                base += count
+
     whole(rep_in, 1).wait_recv()
-
-    parts = [split2(rep_in[:, n, :].T) for n in range(3)]
-    table = jnp.concatenate(
-        [
-            jnp.concatenate([hi for hi, lo in parts], axis=0),
-            jnp.concatenate([lo for hi, lo in parts], axis=0),
-        ],
-        axis=1,
+    table = sources(rep_in, 2)
+    soon_blocks = SOON_PTS // BLK
+    found = []
+    for blk in range(soon_blocks):
+        at = slice(blk * BLK, (blk + 1) * BLK)
+        found.append(pick(table, hot_p[:, at], rankm_p[0:SOON, at], SOON))
+    amplitudes(0, soon_blocks, [jnp.concatenate([row[f] for row in found], axis=1) for f in range(FIELDS)])
+    green(0, SOON_PTS, True, False)
+    whole(rep_in_b, 3).wait_recv()
+    table_b = sources(rep_in_b, 1)
+    found = []
+    for blk in range(soon_blocks, PTS // BLK):
+        at = slice(blk * BLK, (blk + 1) * BLK)
+        found.append(
+            [
+                one + two
+                for one, two in zip(
+                    pick(table, hot_p[:, at], rankm_p[0:SOON, at], SOON),
+                    pick(table_b, hot_p[:, at], rankm_p[SOON:CAP, at], CAP - SOON),
+                )
+            ]
+        )
+    amplitudes(
+        soon_blocks, PTS // BLK, [jnp.concatenate([row[f] for row in found], axis=1) for f in range(FIELDS)]
     )
-    for blk in range(PTS // BLK):
-        at = slice(blk * BLK, (blk + 1) * BLK)
-        candidates = dot_nn(table, hot[:, at])
-        mask = rankm[:, at]
-        for f in range(FIELDS):
-            surf_ref[f : f + 1, at] = jnp.sum(
-                candidates[f * CAP : (f + 1) * CAP, :] * mask, axis=0, keepdims=True
-            )
-
-    density = surf_ref[0:1, :]
-    vel_x = surf_ref[1:2, :]
-    vel_y = surf_ref[2:3, :]
-    vel_z = surf_ref[3:4, :]
-    pressure = surf_ref[4:5, :]
-    normal = vel_x * cos_p + vel_y * sin_p
-    scaled = weight_ref[...] * (1.0 / math.sqrt(PTS * DEV))
-    flux = density * normal * scaled
-    pressure = pressure * scaled
-    left, right = [], []
-    products(left, right, pressure * cos_p + flux * vel_x, obs_x)
-    products(left, right, pressure * sin_p + flux * vel_y, obs_y)
-    products(left, right, flux * vel_z, obs_z)
-    for piece in split3(-(pressure + flux * (normal + vel_z * axial))):
-        left.append(piece.astype(F32))
-        right.append(one_o)
-    zero_o = jnp.zeros((1, NOBS), F32)
-    other = [zero_o] * len(left)
-    for piece in split3(flux):
-        left.append(piece.astype(F32))
-        right.append(zero_o)
-        other.append(one_o)
-    left = jnp.concatenate(left, axis=0).T.astype(BF16)
-    right = jnp.concatenate(
-        [jnp.concatenate(right, axis=0), jnp.concatenate(other, axis=0)], axis=1
-    ).astype(BF16)
-    for blk in range(PTS // BLK):
-        mixed = dot_nn(left[blk * BLK : (blk + 1) * BLK, :], right)
-        for n in range(BLK // 8):
-            at = blk * (BLK // 8) + n
-            for g in range(2):
-                lanes = slice(g * 128, (g + 1) * 128)
-                inv = geo[at, g, 14]
-                linear = mixed[n * 8 : n * 8 + 8, lanes]
-                amp[at, g] = (mixed[n * 8 : n * 8 + 8, 256 + g * 128 : 384 + g * 128] + linear * inv) * (
-                    inv * orad[:, lanes]
-                )
-
-    UNROLL = 8
-    for g in range(2):
-        lanes = slice(g * 128, (g + 1) * 128)
-        for number, (centre, reach) in enumerate(CENTRES):
-
-            def body(step, acc, number=number, reach=reach, g=g):
-                acc = list(acc)
-                for u in range(UNROLL):
-                    blk = step * UNROLL + u
-                    a = amp[blk, g]
-                    at = 4 if number == 0 else 6 + 2 * number
-                    ac = a * geo[blk, g, at]
-                    as_ = a * geo[blk, g, at + 1]
-                    acc[0] = acc[0] + ac
-                    acc[1] = acc[1] + as_
-                    for b in range(reach):
-                        yc = geo[blk, g, 2 * b]
-                        ysn = geo[blk, g, 2 * b + 1]
-                        acc[2 + 4 * b] = acc[2 + 4 * b] + ac * yc
-                        acc[3 + 4 * b] = acc[3 + 4 * b] + as_ * ysn
-                        acc[4 + 4 * b] = acc[4 + 4 * b] + as_ * yc
-                        acc[5 + 4 * b] = acc[5 + 4 * b] + ac * ysn
-                return tuple(acc)
-
-            start = tuple(jnp.zeros((8, 128), F32) for _ in range(2 + 4 * reach))
-            acc = lax.fori_loop(0, PTS // (8 * UNROLL), body, start)
-
-            def put(k, cosine, sine, lanes=lanes):
-                sums[k - 1 : k, lanes] = jnp.sum(cosine, axis=0, keepdims=True)
-                sums[NFREQ + k - 1 : NFREQ + k, lanes] = jnp.sum(sine, axis=0, keepdims=True)
-
-            put(centre, acc[0], acc[1])
-            for b in range(reach):
-                p1, p2, p3, p4 = acc[2 + 4 * b : 6 + 4 * b]
-                put(centre + b + 1, p1 - p2, p3 + p4)
-                put(centre - b - 1, p1 + p2, p3 - p4)
+    green(SOON_PTS, PTS, False, True)
 
     slot = slot_ref[...]
     col_iota = lax.broadcasted_iota(jnp.int32, (DEV, NOBS), 0) * 2
@@ -448,9 +548,15 @@
         choose = jnp.where(col_iota + parity == slot, 1.0, 0.0).astype(BF16)
         placed.append(dot_nt(choose, pieces[0]) + dot_nt(choose, pieces[1]) + dot_nt(choose, pieces[2]))
     red_out[:, 0, :] = jnp.concatenate(placed, axis=1)
-    exchange(red_out, red_in, 2, True)
+    exchange(red_out, red_in, 2, own=True)
     red_in[0] = red_out[me]
     cos_f, sin_f = sincos_twice(phase_ref[...] * 0.5)
+    for blk in range(PTS // BLK):
+        at = slice(blk * BLK, (blk + 1) * BLK)
+        one = pick(table, hot[:, at], rankm[0:SOON, at], SOON)
+        two = pick(table_b, hot[:, at], rankm[SOON:CAP, at], CAP - SOON)
+        for f in range(FIELDS):
+            surf_ref[f : f + 1, at] = one[f] + two[f]
     whole(red_in, 2).wait_recv()
     total = jnp.sum(red_in[:, 0, :], axis=0, keepdims=True)
     for parity in range(2):
@@ -464,6 +570,7 @@
         )
     whole(req_in, 0).wait_send()
     whole(rep_in, 1).wait_send()
+    whole(rep_in_b, 3).wait_send()
     whole(red_in, 2).wait_send()
 
 
@@ -489,7 +596,7 @@
             jax.ShapeDtypeStruct((FIELDS, PTS), F32),
             jax.ShapeDtypeStruct((2, 2, NFREQ), F32),
         ),
-        in_specs=[pl.BlockSpec(memory_space=pl.ANY)] + [vmem] * 12,
+        in_specs=[pl.BlockSpec(memory_space=pltpu.HBM)] + [vmem] * 12,
         out_specs=(vmem, vmem),
         scratch_shapes=[
             pltpu.VMEM((FIELDS, ELEM, NODES), BF16),
@@ -500,9 +607,16 @@
             pltpu.VMEM((DEV, 2, 128), F32),
             pltpu.VMEM((CAP, 128), F32),
             pltpu.VMEM((CAP, 24, 128), F32),
-            pltpu.VMEM((384, 128), F32),
-            pltpu.VMEM((DEV, 3, 128), F32),
-            pltpu.VMEM((DEV, 3, 128), F32),
+            pltpu.VMEM((256, 128), F32),
+            pltpu.VMEM((128, 128), F32),
+            pltpu.VMEM((DEV, 2, 128), F32),
+            pltpu.VMEM((DEV, 2, 128), F32),
+            pltpu.VMEM((DEV, 1, 128), F32),
+            pltpu.VMEM((DEV, 1, 128), F32),
+            pltpu.VMEM((PTS - SOON_PTS, PTS), BF16),
+            pltpu.VMEM((2 * DEV, PTS), BF16),
+            pltpu.VMEM((CAP, PTS), F32),
+            pltpu.VMEM((2, 66, 8, 128), F32),
             pltpu.VMEM((PTS, NOBS), F32),
             pltpu.VMEM((PTS // 8, 2, 8, 128), F32),
             pltpu.VMEM((PTS // 8, 2, 15, 8, 128), F32),
@@ -510,7 +624,7 @@
             pltpu.VMEM((DEV, 1, 128), F32),
             pltpu.VMEM((DEV, 1, 128), F32),
             pltpu.SemaphoreType.DMA,
-            pltpu.SemaphoreType.DMA((6,)),
+            pltpu.SemaphoreType.DMA((8,)),
         ],
         compiler_params=pltpu.CompilerParams(
             collective_id=0, has_side_effects=True, vmem_limit_bytes=63 * 1024 * 1024

time: 72.4 us -> 68 us (0.939)
  Pallas kernels: 68.8 us -> 64.4 us
    pallas_call x1, Pallas kernels: 68.8 us -> 64.4 us  [on_device(): pl.pallas_call(kernel, out_shape=(jax.ShapeDtypeStruct((FIELDS, PTS), F32...]
where the time goes in v3:
time: 68 us; the launch traced here: 67.7 us
  Pallas kernels  64.4 us (95%)
  local copies, waits for them, and re-layouts  2.72 us (4%)
    pallas_call x1, Pallas kernels, on_device(): pl.pallas_call(kernel, out_shape=(jax.ShapeDtypeStruct((FIELDS, PTS), F32...  64.4 us
    unnamed x2, local copies, waits for them, and re-layouts  2.72 us

profile of v3, /device:TPU:1, one launch (start us, length us, event | category | flops | bytes accessed | tf_op | source)
XLA Modules:
  0.0 67.7 jit_solution(10715578244213824267)
XLA Ops:
  0.6 64.4 %flow.1 = (f32[5,2048]{1,0:T(8,128)}, f32[2,2,32]{2,1,0:T(2,128)}) custom-call(bf16[5,512,512]{2,1,0:T(8,128)(2,1)} %bitcast.13, f32[3,2048]{1,0:T(4,128)} %coords_ref.1, s32[1,2048]{1,0:T(1,128)} %bitcast.14, s32[1,2048]{1,0:T(1,128)} %bitcast.15, f32[1,2048]{1,0:T(1,128)} %bitcast.16, f32[1,2048]{1,0:T(1,128)} %bitcast.17, f32[1,2048]{1,0:T(1,128)} %bitcast.18, ...), custom_call_target="tpu_custom_call" | custom-call | tf_op jit(solution)/shard_map/flow/pallas_call | solution.py:593
  65.0 1.5 %copy.17 = f32[5,2048]{1,0:T(8,128)} copy(f32[5,2048]{1,0:T(8,128)} %get-tuple-element.8) | data formatting | bytes 81920
  66.5 1.2 %copy.18 = f32[2,32,2]{1,2,0:T(2,128)} copy(f32[2,32,2]{1,2,0:T(2,128)} %bitcast.20) | data formatting | bytes 1024

commit v4 on v3

--- a/solution.py
+++ b/solution.py
@@ -24,6 +24,8 @@
 BLK = 256
 WIDE = 8
 UNROLL = 16
+EVERY = 1
+INSIDE = PTS // 8 - (20 // EVERY) * (CAP // WIDE)
 SOON = 48
 SOON_PTS = PTS * SOON // CAP
 DELTAS = sorted(
@@ -158,6 +160,7 @@
     req_in,
     rid,
     lag,
+    lag_t,
     valt,
     valt_b,
     rep_out,
@@ -332,9 +335,12 @@
     def geometry(first, last):
         @pl.loop(first, last)
         def _(step):
-            for u in range(2):
-                blk = step * 2 + u
-                for g in range(2):
+            pairs_of([(step * 2 + u, g) for u in range(2) for g in range(2)])
+
+    def pairs_of(places):
+        if True:
+            if True:
+                for blk, g in places:
                     square = square_ref[pl.ds(pl.multiple_of(blk * 8, 8), 8), g * 128 : (g + 1) * 128]
                     inv = lax.rsqrt(square)
                     dist = square * inv
@@ -364,28 +370,33 @@
                     ):
                         geo[blk, g, n] = value
 
-    geometry(0, PTS // 16)
+    geometry(0, INSIDE // 2)
 
     whole(req_in, 0).wait_recv()
 
     first = req_in[:, 0, :].T
     second = req_in[:, 1, :].T
     rid[...] = first[0:CAP]
-    for n, value in enumerate((first[CAP : 2 * CAP], second[0:CAP], second[CAP : 2 * CAP])):
+    for n, value in enumerate((first[CAP : 2 * CAP], second[0:CAP])):
         for i, weight in enumerate(lagrange(value)):
-            lag[:, n * 8 + i, :] = weight
+            lag[n * 8 + i] = weight
+    for i, weight in enumerate(lagrange(second[CAP : 2 * CAP])):
+        lag_t[:, i, :] = weight
 
     elem_iota = lax.broadcasted_iota(jnp.int32, (ELEM, 128), 0).astype(F32)
 
     def gather(group, land, first, span):
         picks = []
         weights = []
+        inner_weights = []
         for part in range(WIDE):
             c = group * WIDE + part
             picks.append(jnp.where(elem_iota == rid[pl.ds(c, 1), :], 1.0, 0.0).astype(BF16))
-            weights.append(lag[c])
+            weights.append([lag[n, pl.ds(c, 1), :] for n in range(16)])
+            inner_weights.append(lag_t[c])
         pick = jnp.concatenate(picks, axis=1)
-        weight = jnp.concatenate(weights, axis=1)
+        weight = [jnp.concatenate([row[n] for row in weights], axis=1) for n in range(16)]
+        inner_weight = jnp.concatenate(inner_weights, axis=1)
         for f in range(FIELDS):
             nodal = dot_nn(tabt[f * NODES : (f + 1) * NODES, :], pick)
             total = None
@@ -393,11 +404,14 @@
                 inner = None
                 for j in range(8):
                     at = (i * 8 + j) * 8
-                    term = nodal[at : at + 8, :] * weight[8 + j : 9 + j, :]
+                    term = nodal[at : at + 8, :] * weight[8 + j]
                     inner = term if inner is None else inner + term
-                inner = inner * weight[i : i + 1, :]
+                inner = inner * weight[i]
                 total = inner if total is None else total + inner
-            value = jnp.sum(total * weight[16:24, :], axis=0, keepdims=True)
+                if i % EVERY == 0:
+                    unit = f * (8 // EVERY) + i // EVERY
+                    pairs_of([(INSIDE + group * (20 // EVERY) + unit // 2, unit % 2)])
+            value = jnp.sum(total * inner_weight, axis=0, keepdims=True)
             for part in range(WIDE):
                 land[pl.ds(f * span + (group * WIDE - first) + part, 1), :] = value[:, part * 128 : (part + 1) * 128]
 
@@ -574,6 +588,17 @@
     whole(red_in, 2).wait_send()
 
 
+def hand_over(surface_in, spectra_in, surface_out, spectra_out, sems):
+    copies = [
+        pltpu.make_async_copy(surface_in, surface_out, sems.at[0]),
+        pltpu.make_async_copy(spectra_in, spectra_out, sems.at[1]),
+    ]
+    for copy in copies:
+        copy.start()
+    for copy in copies:
+        copy.wait()
+
+
 def on_device(
     element_fields,
     ref_coords,
@@ -592,10 +617,7 @@
     vmem = pl.BlockSpec(memory_space=pltpu.VMEM)
     surface, spectra = pl.pallas_call(
         kernel,
-        out_shape=(
-            jax.ShapeDtypeStruct((FIELDS, PTS), F32),
-            jax.ShapeDtypeStruct((2, 2, NFREQ), F32),
-        ),
+        out_shape=(pltpu.VMEM((FIELDS, PTS), F32), pltpu.VMEM((2, 2, NFREQ), F32)),
         in_specs=[pl.BlockSpec(memory_space=pltpu.HBM)] + [vmem] * 12,
         out_specs=(vmem, vmem),
         scratch_shapes=[
@@ -606,7 +628,8 @@
             pltpu.VMEM((DEV, 2, 128), F32),
             pltpu.VMEM((DEV, 2, 128), F32),
             pltpu.VMEM((CAP, 128), F32),
-            pltpu.VMEM((CAP, 24, 128), F32),
+            pltpu.VMEM((16, CAP, 128), F32),
+            pltpu.VMEM((CAP, 8, 128), F32),
             pltpu.VMEM((256, 128), F32),
             pltpu.VMEM((128, 128), F32),
             pltpu.VMEM((DEV, 2, 128), F32),
@@ -645,6 +668,20 @@
         observer_slot.reshape(1, NOBS),
         prior_spectra.transpose(0, 2, 1),
     )
+    surface, spectra = pl.pallas_call(
+        hand_over,
+        out_shape=(
+            jax.ShapeDtypeStruct((FIELDS, PTS), F32),
+            jax.ShapeDtypeStruct((2, 2, NFREQ), F32),
+        ),
+        in_specs=[vmem, vmem],
+        out_specs=(pl.BlockSpec(memory_space=pltpu.HBM), pl.BlockSpec(memory_space=pltpu.HBM)),
+        scratch_shapes=[pltpu.SemaphoreType.DMA((2,))],
+        name="hand_over",
+    )(
+        pltpu.with_memory_space_constraint(surface, pltpu.VMEM),
+        pltpu.with_memory_space_constraint(spectra, pltpu.VMEM),
+    )
     return surface, spectra.transpose(0, 2, 1)
 
 

time: 68 us -> 64.5 us (0.949)
  local copies, waits for them, and re-layouts: 2.72 us -> 0 us
  Pallas kernels: 64.4 us -> 63.5 us
    unnamed x2 -> x0, local copies, waits for them, and re-layouts: 2.72 us -> none
    pallas_call x1 -> x2, Pallas kernels: 64.4 us -> 63.5 us  [the longest x1 62.9 us: on_device(): pl.pallas_call(kernel, out_shape=(pltpu.VMEM((FIELDS, PTS), F32), pltpu.V...]
where the time goes in v4:
time: 64.5 us; the launch traced here: 64.3 us
  Pallas kernels  63.5 us (98%)
  between operations  0.8 us (1%)
    pallas_call x1, Pallas kernels, on_device(): pl.pallas_call(kernel, out_shape=(pltpu.VMEM((FIELDS, PTS), F32), pltpu.V...  62.9 us

profile of v4, /device:TPU:1, one launch (start us, length us, event | category | flops | bytes accessed | tf_op | source)
XLA Modules:
  0.0 64.3 jit_solution(10509651914193911499)
XLA Ops:
  0.6 62.9 %flow.1 = (f32[5,2048]{1,0:T(8,128)S(1)}, f32[2,2,32]{2,1,0:T(2,128)S(1)}) custom-call(bf16[5,512,512]{2,1,0:T(8,128)(2,1)} %bitcast.13, f32[3,2048]{1,0:T(4,128)} %coords_ref.1, s32[1,2048]{1,0:T(1,128)} %bitcast.14, s32[1,2048]{1,0:T(1,128)} %bitcast.15, f32[1,2048]{1,0:T(1,128)} %bitcast.16, f32[1,2048]{1,0:T(1,128)} %bitcast.17, f32[1,2048]{1,0:T(1,128)} %bitcast.18, ...), custom_call_target="tpu_custom_call" | custom-call | tf_op jit(solution)/shard_map/flow/pallas_call | solution.py:618
  63.5 0.7 %hand_over.1 = (f32[5,2048]{1,0:T(8,128)}, f32[2,2,32]{2,1,0:T(2,128)}) custom-call(f32[5,2048]{1,0:T(8,128)S(1)} %get-tuple-element.6.surface_in, f32[2,2,32]{2,1,0:T(2,128)S(1)} %get-tuple-element.7.spectra_in), custom_call_target="tpu_custom_call" | custom-call | tf_op jit(solution)/shard_map/hand_over/pallas_call | solution.py:671

commit v5 on v4

--- a/solution.py
+++ b/solution.py
@@ -281,6 +281,10 @@
     req_out[:, 0, :] = packed[:, 0:128]
     req_out[:, 1, :] = packed[:, 128:256]
 
+    pl.semaphore_wait(barrier, DEV - 1)
+    exchange(req_out, req_in, 0)
+    req_in[0] = req_out[0]
+
     cos_p, sin_p = sincos_twice(angle_ref[...] * 0.5)
     attributes = [piece.astype(F32) for row in (cos_p, sin_p, axial_ref[...], weight_ref[...]) for piece in split3(row)]
     attributes.append(rel.astype(F32))
@@ -304,10 +308,6 @@
         hot_p[0:DEV, at] = onehot16
         hot_p[DEV : 2 * DEV, at] = onehot16
         rankm_p[:, at] = jnp.where(cap_iota == rank_p[:, at], 1.0, 0.0)
-
-    pl.semaphore_wait(barrier, DEV - 1)
-    exchange(req_out, req_in, 0)
-    req_in[0] = req_out[0]
 
     cos_o, sin_o = sincos_twice(oang_ref[...] * 0.5)
     orad = orad_ref[...]

time: 64.5 us -> 64.5 us (level)
  no operation moved by 1% of the time
where the time goes in v5:
time: 64.5 us; the launch traced here: 64.3 us
  Pallas kernels  63.5 us (98%)
  between operations  0.8 us (1%)
    pallas_call x1, Pallas kernels, on_device(): pl.pallas_call(kernel, out_shape=(pltpu.VMEM((FIELDS, PTS), F32), pltpu.V...  62.9 us

profile of v5, /device:TPU:1, one launch (start us, length us, event | category | flops | bytes accessed | tf_op | source)
XLA Modules:
  0.0 64.3 jit_solution(4721613454394371908)
XLA Ops:
  0.6 62.9 %flow.1 = (f32[5,2048]{1,0:T(8,128)S(1)}, f32[2,2,32]{2,1,0:T(2,128)S(1)}) custom-call(bf16[5,512,512]{2,1,0:T(8,128)(2,1)} %bitcast.13, f32[3,2048]{1,0:T(4,128)} %coords_ref.1, s32[1,2048]{1,0:T(1,128)} %bitcast.14, s32[1,2048]{1,0:T(1,128)} %bitcast.15, f32[1,2048]{1,0:T(1,128)} %bitcast.16, f32[1,2048]{1,0:T(1,128)} %bitcast.17, f32[1,2048]{1,0:T(1,128)} %bitcast.18, ...), custom_call_target="tpu_custom_call" | custom-call | tf_op jit(solution)/shard_map/flow/pallas_call | solution.py:618
  63.5 0.7 %hand_over.1 = (f32[5,2048]{1,0:T(8,128)}, f32[2,2,32]{2,1,0:T(2,128)}) custom-call(f32[5,2048]{1,0:T(8,128)S(1)} %get-tuple-element.6.surface_in, f32[2,2,32]{2,1,0:T(2,128)S(1)} %get-tuple-element.7.spectra_in), custom_call_target="tpu_custom_call" | custom-call | tf_op jit(solution)/shard_map/hand_over/pallas_call | solution.py:671
